TPU v7x, 32 devices: a whole 2x2x4 slice. The times are simulated.
32 devices in a mesh: context: 2 (over core), tensor: 4 (over y, x), fsdp: 4 (over z).
Axes of the slice: x: 2, y: 2, z: 4, core: 2. Of those that a mesh axis runs over, the one named last changes fastest.
Arguments:
- input_raw: bfloat16 [4, 1024, 5120], P('fsdp', ('context', 'tensor')), may hold values from -6 to 6
- state_proj_raw: bfloat16 [4, 1024, 256], P('fsdp', ('context', 'tensor')), may hold values from -6 to 6
- gate_branch: bfloat16 [4, 1024, 5120], P('fsdp', ('context', 'tensor')), may hold values from -6 to 6
- step_raw: bfloat16 [4, 1024, 80], P('fsdp', ('context', 'tensor')), may hold values from -6 to 6
- convolution_taps: float32 [4, 5376], replicated, may hold values from -3 to 3
- convolution_bias: float32 [5376], replicated, may hold values from -3 to 3
- step_bias: float32 [80], P('tensor'), may hold values from -1.5 to 0.5
- decay_log_rate: float32 [80], P('tensor'), may hold values from -13 to -2, as said below
- skip_weight: float32 [80], P('tensor'), may hold values from 0.5 to 2
- gated_norm_gain: float32 [5120], P('tensor'), may hold values from 0.1 to 1.9
- output_weight: bfloat16 [5120, 2560], P('tensor', 'fsdp'), may hold values from -0.078125 to 0.078125
- adapter_down: bfloat16 [5120, 16], P('tensor'), may hold values from -0.078125 to 0.078125
- adapter_up: bfloat16 [16, 2560], replicated, may hold values from -0.29882812 to 0.29882812
- cotangent: bfloat16 [4, 1024, 2560], P('fsdp', ('context', 'tensor')), may hold values from -6 to 6
Outputs:
- mixed: bfloat16 [4, 1024, 2560], P('fsdp', ('context', 'tensor'))
- grad_a: float32 [5120, 16], P('tensor')
- grad_b: float32 [16, 2560], replicated
Inputs may be any that keep to these rules, and one draw needn't show every extreme that they name: `decay_log_rate`: logarithms of positive decay rates.
All inputs are finite; a program needn't handle non-finite values.
Results may differ from a plain program's by a relative error of at most 0.017.
Values may be sent and summed in bfloat16 or wider, within the bound.
No kernel may reach another device: no remote copies, remote signals or barrier semaphores. Data moves between devices by JAX's collectives and lax.ppermute only.
A program may use at most 128 MiB of HBM per device.

v0:
```python
import math

import jax
import jax.numpy as jnp
from jax import lax
from jax.sharding import PartitionSpec as P

epsilon = 1e-05


def passed_along(value, axis, steps):
    count = lax.axis_size(axis)
    leading, last = (max(0, -steps), min(count, count - steps))
    return lax.ppermute(value, axis, [(source, source + steps) for source in range(leading, last)])


def entering(value, axis, join, neutral):
    count, mine = (lax.axis_size(axis), lax.axis_index(axis))
    pieces = jax.tree.map(lambda part: lax.all_gather(part, axis), value)
    subtotal = jax.tree.map(
        lambda part, zero: jnp.full_like(part, 0) + jnp.asarray(zero, part.dtype), value, neutral
    )

    def lap(position, subtotal):
        longer = join(subtotal, jax.tree.map(lambda part: part[position], pieces))
        return jax.tree.map(lambda new, old: jnp.where(position < mine, new, old), longer, subtotal)

    return lax.fori_loop(0, count - 1, lap, subtotal)


def convolve(values, before, weight, bias_row):
    length = values.shape[0]
    extended = jnp.concatenate([before, values], axis=0)
    pre_act = bias_row[None, :] + weight[0][None, :] * extended[0:length].astype(jnp.float32)
    for tap_index in range(1, weight.shape[0]):
        pre_act = pre_act + weight[tap_index][None, :] * extended[
            tap_index : tap_index + length
        ].astype(jnp.float32)
    return jax.nn.silu(pre_act).astype(jnp.bfloat16)


def ssd_blocks(x_heads, b_rows, c_rows, step_size, log_decay, block_len):
    highest = lax.Precision.HIGHEST
    length = x_heads.shape[0]
    head_count = x_heads.shape[1]
    head_size = x_heads.shape[2]
    state_size = b_rows.shape[1]
    blocks = length // block_len
    causal = jnp.arange(block_len)[:, None] >= jnp.arange(block_len)[None, :]

    def advance(state_now, pieces):
        x_block, b_block, c_block, step_block, decay_block = pieces
        cum_decay = jnp.cumsum(decay_block, axis=0)
        cum_heads = cum_decay.T
        gap_decay = cum_heads[:, :, None] - cum_heads[:, None, :]
        decay_mat = jnp.where(causal[None], jnp.exp(jnp.where(causal[None], gap_decay, 0.0)), 0.0)
        gram_mat = jnp.dot(c_block, b_block.T, precision=highest)
        x_scaled = x_block * step_block[:, :, None]
        y_inner = jnp.einsum(
            "hij,jhp->ihp", decay_mat * gram_mat[None], x_scaled, precision=highest
        )
        y_state = jnp.exp(cum_decay)[:, :, None] * jnp.einsum(
            "in,hpn->ihp", c_block, state_now, precision=highest
        )
        tail_decay = jnp.exp(cum_decay[-1][None, :] - cum_decay)
        state_next = jnp.exp(cum_decay[-1])[:, None, None] * state_now + jnp.einsum(
            "jhp,jn->hpn", x_scaled * tail_decay[:, :, None], b_block, precision=highest
        )
        return (state_next, y_inner + y_state)

    start_state = jnp.zeros((head_count, head_size, state_size), jnp.float32)
    state_end, y_blocks = lax.scan(
        advance,
        start_state,
        (
            x_heads.reshape(blocks, block_len, head_count, head_size),
            b_rows.reshape(blocks, block_len, state_size),
            c_rows.reshape(blocks, block_len, state_size),
            step_size.reshape(blocks, block_len, head_count),
            log_decay.reshape(blocks, block_len, head_count),
        ),
    )
    return (y_blocks.reshape(length, head_count, head_size), state_end)


def chain_states(earlier, later):
    return (earlier[0] + later[0], jnp.exp(later[0])[:, None, None] * earlier[1] + later[1])


def row_slice(values, start_row, row_count):
    return lax.dynamic_slice_in_dim(values, start_row, row_count, 0)


def shards(
    input_raw,
    state_proj_raw,
    gate_branch,
    step_raw,
    convolution_taps,
    convolution_bias,
    step_bias,
    decay_log_rate,
    skip_weight,
    gated_norm_gain,
    output_weight,
    adapter_down,
    adapter_up,
    cotangent,
):
    highest = lax.Precision.HIGHEST
    tok_rows = input_raw.shape[1]
    inner_width = input_raw.shape[2]
    state_size = state_proj_raw.shape[2] // 2
    rim_width = convolution_taps.shape[0] - 1
    joined = jnp.concatenate([input_raw[0], state_proj_raw[0]], axis=1)
    before = passed_along(joined[tok_rows - rim_width :], ("context", "tensor"), 1)
    convolved = convolve(joined, before, convolution_taps, convolution_bias)
    x_heads_raw, z_heads, dt_heads = (
        lax.all_to_all(
            convolved[:, :inner_width], "tensor", split_axis=1, concat_axis=0, tiled=True
        ),
        lax.all_to_all(gate_branch[0], "tensor", split_axis=1, concat_axis=0, tiled=True),
        lax.all_to_all(step_raw[0], "tensor", split_axis=1, concat_axis=0, tiled=True),
    )
    shared = lax.all_gather(convolved[:, inner_width:], "tensor", axis=0, tiled=True)
    span_rows = x_heads_raw.shape[0]
    local_heads = dt_heads.shape[1]
    local_width = x_heads_raw.shape[1]
    head_size = local_width // local_heads
    x_heads = x_heads_raw.astype(jnp.float32).reshape(span_rows, local_heads, head_size)
    b_rows = shared[:, :state_size].astype(jnp.float32)
    c_rows = shared[:, state_size:].astype(jnp.float32)
    step_size = jax.nn.softplus(dt_heads.astype(jnp.float32) + step_bias[None, :])
    log_decay = -step_size * jnp.exp(decay_log_rate)[None, :]
    y_local, state_end = ssd_blocks(
        x_heads, b_rows, c_rows, step_size, log_decay, math.gcd(span_rows, 256)
    )
    log_total = jnp.sum(log_decay, axis=0)
    prior_total, incoming = entering(
        (log_total, state_end),
        "context",
        chain_states,
        (jnp.zeros_like(log_total), jnp.zeros_like(state_end)),
    )
    reach_decay = jnp.exp(jnp.cumsum(log_decay, axis=0))
    y_heads = y_local + reach_decay[:, :, None] * jnp.einsum(
        "tn,hpn->thp", c_rows, incoming, precision=highest
    )
    y_heads = y_heads + skip_weight[None, :, None] * x_heads
    gated = y_heads.reshape(span_rows, local_width) * jax.nn.silu(z_heads.astype(jnp.float32))
    squares = jnp.sum(gated * gated, axis=1)
    gated_output = (gated * gated_norm_gain[None, :]).astype(jnp.bfloat16)
    adapter_piece = jnp.dot(gated_output, adapter_down, preferred_element_type=jnp.float32)
    full_width = local_width * lax.axis_size("tensor")
    columns = lax.all_gather(output_weight, "fsdp", axis=1, tiled=True)
    own_start = lax.axis_index("tensor") * tok_rows
    sum_squares, adapter_all = (
        lax.psum(squares.astype(jnp.bfloat16), "tensor").astype(jnp.float32),
        lax.psum(adapter_piece.astype(jnp.bfloat16), "tensor").astype(jnp.float32),
    )
    scale_all = lax.rsqrt(sum_squares / full_width + epsilon)
    adapter_all = adapter_all.astype(jnp.bfloat16)
    leader = (lax.axis_index("tensor") == 0).astype(jnp.float32)
    start_row = jnp.int32(0)
    frozen_piece = jnp.dot(
        row_slice(gated_output, start_row, lax.axis_size("tensor") * tok_rows),
        columns,
        preferred_element_type=jnp.float32,
    )
    frozen_piece = frozen_piece + 2.0 * leader * jnp.dot(
        row_slice(adapter_all, start_row, lax.axis_size("tensor") * tok_rows),
        adapter_up,
        preferred_element_type=jnp.float32,
    )
    summed = lax.psum_scatter(
        (
            row_slice(scale_all, start_row, lax.axis_size("tensor") * tok_rows)[:, None]
            * frozen_piece
        ).astype(jnp.bfloat16),
        "tensor",
        scatter_dimension=0,
        tiled=True,
    )
    row_norm_scale = row_slice(scale_all, own_start, tok_rows)
    adapter_branch = row_slice(adapter_all, own_start, tok_rows)
    cotangent_rows = cotangent[0]
    token_total = (
        tok_rows * lax.axis_size("context") * lax.axis_size("tensor") * lax.axis_size("fsdp")
    )
    lowrank_factor = 2.0 / math.sqrt(token_total)
    weighted = lowrank_factor * row_norm_scale[:, None] * adapter_branch.astype(jnp.float32)
    grad_b_local = jnp.dot(weighted.T, cotangent_rows.astype(jnp.float32), precision=highest)
    adapter_gradient = (
        lowrank_factor
        * row_norm_scale[:, None]
        * jnp.dot(cotangent_rows, adapter_up.T, preferred_element_type=jnp.float32)
    )
    adapter_span = lax.all_gather(adapter_gradient, "tensor", axis=0, tiled=True)
    grad_a_local = jnp.dot(gated_output.astype(jnp.float32).T, adapter_span, precision=highest)
    grad_a, grad_b_part = lax.psum((grad_a_local, grad_b_local), ("context", "fsdp"))
    grad_b = lax.psum(grad_b_part.astype(jnp.bfloat16), "tensor").astype(jnp.float32)
    return (summed[None], grad_a, grad_b)


def solution(mesh):
    placed = (
        P("fsdp", ("context", "tensor"), None),
        P("fsdp", ("context", "tensor"), None),
        P("fsdp", ("context", "tensor"), None),
        P("fsdp", ("context", "tensor"), None),
        P(),
        P(),
        P("tensor"),
        P("tensor"),
        P("tensor"),
        P("tensor"),
        P("tensor", "fsdp"),
        P("tensor", None),
        P(),
        P("fsdp", ("context", "tensor"), None),
    )
    return jax.shard_map(
        shards,
        mesh=mesh,
        in_specs=placed,
        out_specs=(P("fsdp", ("context", "tensor"), None), P("tensor", None), P()),
        check_vma=False,
    )
```

profile of v0, /device:TPU:0, one launch (start us, length us, event | category | flops | bytes accessed | tf_op | source)
XLA Modules:
  0.0 443.3 jit_solution(7496762377417726398)
XLA Ops:
  8.3 4.9 %collective-permute-start = (bf16[3,5376]{1,0:T(4,128)(2,1)S(1)}, bf16[3,5376]{1,0:T(4,128)(2,1)S(1)}, u32[]{:S(2)}, u32[]{:S(2)}) collective-permute-start(bf16[3,5376]{1,0:T(4,128)(2,1)S(1)} %fusion.75), channel_id=1, source_target_pairs={{0,4},{4,8},{8,12},{12,16},{16,20},{20,24},{24,28},{1,5},{5,9},{9,... | collective-permute-start | bytes 96776 | tf_op jit(solution)/shard_map/ppermute | solution.py:14
  14.5 3.3 all-to-all-start
  24.6 4.2 all-to-all-start.1
  30.3 19.2 %all_gather.21 = bf16[512,256]{1,0:T(8,128)(2,1)S(1)} all-gather(bf16[128,256]{1,0:T(8,128)(2,1)S(1)} %slice.84), channel_id=1, replica_groups=mesh['context'=2,'tensor'=4,'fsdp'=4] {'tensor'}, dimensions={0}, use_global_device_ids=true | all-gather | bytes 327680 | tf_op jit(solution)/shard_map/all_gather | solution.py:125
  51.1 5.4 %copy.68 = f32[4,128,1280]{1,0,2:T(4,128)S(1)} copy(f32[4,128,1280]{1,2,0:T(8,128)S(1)} %convert_bitcast_fusion.1) | data formatting | bytes 5242880 | tf_op jit(solution)/shard_map/convert_element_type | solution.py:130
  56.5 3.4 reshape.159
  59.9 93.5 %while.4 = (s32[]{:T(128)}, f32[20,64,128]{2,1,0:T(8,128)}, f32[2,256,20,64]{1,0,3,2:T(2,128)}, f32[2,256,20]{1,0,2:T(2,128)}, f32[2,256,20,64]{1,0,3,2:T(2,128)...) while((s32[]{:T(128)}, f32[20,64,128]{2,1,0:T(8,128)}, ...), condition=%wide.region_3.4_spmd.clone.clone, body=%wide.region_0.3_spmd.clone.clone.sunk | while | flops 2122191872 | bytes 18280176 | solution.py:72
  63.0 3.1 constant_dynamic-slice_fusion.5
  66.2 6.0 %fusion.115 = f32[256,20,64]{0,2,1:T(8,128)S(1)} fusion(f32[256,256]{1,0:T(8,128)S(1)} %fusion.114, f32[20,256]{1,0:T(8,128)S(1)} %bitcast.176, pred[256,256]{1,0:T(8,128)(4,1)S(1)} %iota_compare_fusion.2, f32[1,256,20,64]{1,0,3,2:T(1,128)S(1)} %constant_dynamic-slice_fusion.5, f32[256,20]{0,1:T(8,128)S(1)} %bitcast.180), kind=kOutput, calls=%fused_computation.15.clone.1 | convolution fusion | flops 1012203520 | bytes 2990080 | tf_op jit(solution)/shard_map/while/body/eval_jaxpr/hij,jhp->ihp/dot_general | solution.py:59
  76.5 27.0 %dynamic_update_slice.7 = f32[2,256,20,64]{1,0,3,2:T(2,128)} dynamic-update-slice(f32[2,256,20,64]{1,0,3,2:T(2,128)} %get-tuple-element.267, f32[1,256,20,64]{1,0,3,2:T(1,128)S(1)} %copy.124, s32[]{:T(128)} %get-tuple-element.265, s32[]{:T(128)} %constant.41.clone.1..sunk, s32[]{:T(128)} %constant.41.clone.1..sunk, s32[]{:T(128)} %constant.41.clone.1..sunk) | dynamic-update-slice | bytes 2621444 | tf_op jit(solution)/shard_map/while/body/jit(dynamic_update_index_in_dim)/dynamic_update_slice | solution.py:72
  103.6 2.8 fusion.113
  109.5 3.1 constant_dynamic-slice_fusion.5
  112.7 6.0 %fusion.115 = f32[256,20,64]{0,2,1:T(8,128)S(1)} fusion(f32[256,256]{1,0:T(8,128)S(1)} %fusion.114, f32[20,256]{1,0:T(8,128)S(1)} %bitcast.176, pred[256,256]{1,0:T(8,128)(4,1)S(1)} %iota_compare_fusion.2, f32[1,256,20,64]{1,0,3,2:T(1,128)S(1)} %constant_dynamic-slice_fusion.5, f32[256,20]{0,1:T(8,128)S(1)} %bitcast.180), kind=kOutput, calls=%fused_computation.15.clone.1 | convolution fusion | flops 1012203520 | bytes 2990080 | tf_op jit(solution)/shard_map/while/body/eval_jaxpr/hij,jhp->ihp/dot_general | solution.py:59
  123.3 27.0 %dynamic_update_slice.7 = f32[2,256,20,64]{1,0,3,2:T(2,128)} dynamic-update-slice(f32[2,256,20,64]{1,0,3,2:T(2,128)} %get-tuple-element.267, f32[1,256,20,64]{1,0,3,2:T(1,128)S(1)} %copy.124, s32[]{:T(128)} %get-tuple-element.265, s32[]{:T(128)} %constant.41.clone.1..sunk, s32[]{:T(128)} %constant.41.clone.1..sunk, s32[]{:T(128)} %constant.41.clone.1..sunk) | dynamic-update-slice | bytes 2621444 | tf_op jit(solution)/shard_map/while/body/jit(dynamic_update_index_in_dim)/dynamic_update_slice | solution.py:72
  150.3 3.2 fusion.113
  156.2 3.5 all-to-all-start.2
  164.1 2.4 all-reduce
  166.6 6.9 %all-to-all-done.2 = bf16[128,4,1280]{0,2,1:T(8,128)(2,1)S(1)} async-done(((bf16[128,4,1280]{0,2,1:T(8,128)(2,1)}), bf16[128,4,1280]{0,2,1:T(8,128)(2,1)S(1)}, u32[]{:S(2)}, u32[]{:S(2)}) %all-to-all-start.2) | async-done | bytes 1310752 | tf_op jit(solution)/shard_map/all_to_all | solution.py:122
  176.1 4.3 copy.79
  180.4 4.3 reshape.166
  186.8 4.9 %reshape.152 = f32[512,20,64]{0,2,1:T(8,128)} reshape(f32[2,256,20,64]{1,0,3,2:T(2,128)} %get-tuple-element.72) | data formatting | bytes 5242880 | tf_op jit(solution)/shard_map/reshape | solution.py:83
  191.8 6.3 %multiply_reduce_fusion = (bf16[512]{0:T(512)(128)(2,1)S(1)}, f32[512,20,64]{0,2,1:T(8,128)}) fusion(f32[512,20,64]{0,2,1:T(8,128)S(1)} %copy-done.6, f32[512,20,64]{0,2,1:T(8,128)} %reshape.165, f32[20]{0:T(128)S(1)} %copy-done.22, f32[512,20,64]{0,2,1:T(8,128)} %reshape.152, f32[40,64,128]{2,1,0:T(8,128)} %all-gather.7.cloned.1.call-done, ...), kind=kOutput, calls=%fused_computation.66 | convolution fusion | flops 1014169088 | bytes 11323393 | tf_op jit(solution)/shard_map/tn,hpn->thp/dot_general | solution.py:146
  198.1 3.4 copy.80
  201.5 2.7 fusion.52
  204.7 15.3 %all-reduce.1 = (bf16[512,16]{0,1:T(8,128)(2,1)S(1)}, bf16[512]{0:T(512)(128)(2,1)S(1)}) all-reduce(bf16[512,16]{0,1:T(8,128)(2,1)S(1)} %convolution_convert_fusion, bf16[512]{0:T(512)(128)(2,1)S(1)} %get-tuple-element.195), channel_id=1, replica_groups=mesh['context'=2,'tensor'=4,'fsdp'=4] {'tensor'}, use_global_device_ids=true, to_apply=%region_9.10 | all-reduce | flops 8704 | bytes 34816 | tf_op jit(solution)/shard_map/psum | solution.py:159
  220.6 8.2 %all_gather.27 = f32[512,16]{0,1:T(8,128)S(1)} all-gather(f32[128,16]{0,1:T(8,128)S(1)} %convolution_multiply_fusion.1), channel_id=1, replica_groups=mesh['context'=2,'tensor'=4,'fsdp'=4] {'tensor'}, dimensions={0}, use_global_device_ids=true | all-gather | bytes 40960 | tf_op jit(solution)/shard_map/all_gather | solution.py:198
  228.8 51.7 %all-reduce.9 = bf16[16,2560]{1,0:T(8,128)(2,1)} all-reduce(f32[16,2560]{1,0:T(8,128)S(1)} %fusion.55), channel_id=1, replica_groups=mesh['context'=2,'tensor'=4,'fsdp'=4] {'context','fsdp'}, use_global_device_ids=true, to_apply=%region_12.13 | all-reduce | flops 40960 | bytes 245760 | tf_op jit(solution)/shard_map/psum | solution.py:200
  282.0 9.7 %all-gather.5.cloned.1.call-done = bf16[1280,2560]{1,0:T(8,128)(2,1)} async-done(((bf16[1280,640]{1,0:T(8,128)(2,1)}), bf16[1280,2560]{1,0:T(8,128)(2,1)}) %all-gather.5.cloned.1.call-update) | async-done | bytes 6553616 | tf_op jit(solution)/shard_map/all_gather | solution.py:155
  291.6 5.7 %fusion.84 = f32[512,2560]{1,0:T(8,128)S(1)} fusion(bf16[512,1280]{1,0:T(8,128)(2,1)S(1)} %fusion.52, bf16[1280,2560]{1,0:T(8,128)(2,1)} %all-gather.5.cloned.1.call-done), kind=kOutput, calls=%fused_computation.121 | convolution fusion | flops 3355443200 | bytes 13107200 | tf_op jit(solution)/shard_map/dot_general | solution.py:165
  299.8 35.1 %all-reduce.8.cloned.1.call-done = bf16[16,2560]{1,0:T(8,128)(2,1)} async-done(((bf16[16,2560]{1,0:T(8,128)(2,1)}), bf16[16,2560]{1,0:T(8,128)(2,1)}) %all-reduce.8.cloned.1.call-update) | async-done | bytes 81936 | tf_op jit(solution)/shard_map/psum | solution.py:201
  336.4 52.5 %all-reduce.6.cloned.1.call-done = f32[1280,16]{0,1:T(8,128)} async-done(((f32[1280,16]{0,1:T(8,128)}), f32[1280,16]{0,1:T(8,128)}) %all-reduce.6.cloned.1.call-update) | async-done | bytes 81936 | tf_op jit(solution)/shard_map/psum | solution.py:200
  388.9 46.4 %reduce-scatter.2.cloned.1.call-done = bf16[128,2560]{1,0:T(8,128)(2,1)} async-done(((bf16[512,2560]{1,0:T(8,128)(2,1)}), bf16[128,2560]{1,0:T(8,128)(2,1)}) %reduce-scatter.2.cloned.1.call-update) | async-done | bytes 655376 | tf_op jit(solution)/shard_map/reduce_scatter | solution.py:175
  (155 shorter events, 46.5 us)
Async XLA Ops:
  7.2 212.8 %copy-start = (bf16[1,128,2560]{2,1,0:T(8,128)(2,1)S(1)}, bf16[1,128,2560]{2,1,0:T(8,128)(2,1)}, u32[]{:S(2)}) copy-start(bf16[1,128,2560]{2,1,0:T(8,128)(2,1)} %param.29) | copy-start | bytes 1966084
  7.2 13.6 %copy-start.5 = (bf16[1,128,5120]{2,1,0:T(8,128)(2,1)S(1)}, bf16[1,128,5120]{2,1,0:T(8,128)(2,1)}, u32[]{:S(2)}) copy-start(bf16[1,128,5120]{2,1,0:T(8,128)(2,1)} %param.16) | copy-start | bytes 3932164
  7.2 13.6 %copy-start.11 = (bf16[1,128,256]{2,1,0:T(8,128)(2,1)S(1)}, bf16[1,128,256]{2,1,0:T(8,128)(2,1)}, u32[]{:S(2)}) copy-start(bf16[1,128,256]{2,1,0:T(8,128)(2,1)} %param.17) | copy-start | bytes 196612
  7.2 13.6 %copy-start.18 = (f32[5376]{0:T(1024)S(1)}, f32[5376]{0:T(1024)}, u32[]{:S(2)}) copy-start(f32[5376]{0:T(1024)} %param.21) | copy-start | bytes 64516
  8.3 10.8 %collective-permute-start = (bf16[3,5376]{1,0:T(4,128)(2,1)S(1)}, bf16[3,5376]{1,0:T(4,128)(2,1)S(1)}, u32[]{:S(2)}, u32[]{:S(2)}) collective-permute-start(bf16[3,5376]{1,0:T(4,128)(2,1)S(1)} %fusion.75), channel_id=1, source_target_pairs={{0,4},{4,8},{8,12},{12,16},{16,20},{20,24},{24,28},{1,5},{5,9},{9,... | collective-permute-start | bytes 96776 | tf_op jit(solution)/shard_map/ppermute | solution.py:14
  14.5 10.1 %all-to-all-start = ((bf16[128,4,20]{0,2,1:T(8,128)(2,1)}), bf16[128,4,20]{0,2,1:T(8,128)(2,1)S(1)}, u32[]{:S(2)}, u32[]{:S(2)}) async-start(bf16[128,4,20]{0,2,1:T(8,128)(2,1)} %all_to_all.30), calls=%async_computation | async-start | bytes 49152 | tf_op jit(solution)/shard_map/all_to_all | solution.py:123
  23.1 5.7 %copy-start.21 = (f32[20]{0:T(128)S(1)}, f32[20]{0:T(128)}, u32[]{:S(2)}) copy-start(f32[20]{0:T(128)} %param.23) | copy-start | bytes 244
  23.1 6.4 %copy-start.20 = (f32[20]{0:T(128)S(1)}, f32[20]{0:T(128)}, u32[]{:S(2)}) copy-start(f32[20]{0:T(128)} %param.22) | copy-start | bytes 244
  24.6 4.2 copy-start.15
  24.6 26.3 %all-to-all-start.1 = ((bf16[128,4,1280]{0,2,1:T(8,128)(2,1)}), bf16[128,4,1280]{0,2,1:T(8,128)(2,1)S(1)}, u32[]{:S(2)}, u32[]{:S(2)}) async-start(bf16[128,4,1280]{0,2,1:T(8,128)(2,1)} %bitcast.3), calls=%async_computation.1 | async-start | bytes 2621440 | tf_op jit(solution)/shard_map/all_to_all | solution.py:119
  28.7 163.0 %all-gather.7.cloned.1.call-start = ((), (), s32[]{:S(2)}) async-start(), calls=%async_computation.8 | async-start | bytes 1966080 | tf_op jit(solution)/shard_map/all_gather | solution.py:19
  56.5 3.4 copy-start.1
  63.0 9.1 %copy-start.7 = (f32[1,256,20]{1,2,0:T(8,128)}, f32[1,256,20]{1,2,0:T(8,128)S(1)}, u32[]{:S(2)}) copy-start(f32[1,256,20]{1,2,0:T(8,128)S(1)} %copy.123) | copy-start | bytes 61444 | tf_op jit(solution)/shard_map/while
  109.5 9.1 %copy-start.7 = (f32[1,256,20]{1,2,0:T(8,128)}, f32[1,256,20]{1,2,0:T(8,128)S(1)}, u32[]{:S(2)}) copy-start(f32[1,256,20]{1,2,0:T(8,128)S(1)} %copy.123) | copy-start | bytes 61444 | tf_op jit(solution)/shard_map/while
  153.5 1.3 copy-start.8
  153.5 138.1 %all-gather.5.cloned.1.call-start = ((), (), s32[]{:S(2)}) async-start(), calls=%async_computation.4 | async-start | bytes 8192000 | tf_op jit(solution)/shard_map/all_gather | solution.py:155
  154.8 5.1 %copy-start.23 = (u32[32]{0:T(128)S(1)}, u32[32]{0:T(128)}, u32[]{:S(2)}) copy-start(u32[32]{0:T(128)} %constant.76) | copy-start | bytes 388
  154.8 6.3 %copy-start.13 = (f32[4,128,20]{1,2,0:T(8,128)S(1)}, f32[4,128,20]{1,2,0:T(8,128)}, u32[]{:S(2)}) copy-start(f32[4,128,20]{1,2,0:T(8,128)} %copy-done.12) | copy-start | bytes 122884
  154.8 8.9 %copy-start.16 = (bf16[128,4,20]{0,2,1:T(8,128)(2,1)S(1)}, bf16[128,4,20]{0,2,1:T(8,128)(2,1)}, u32[]{:S(2)}) copy-start(bf16[128,4,20]{0,2,1:T(8,128)(2,1)} %copy-done.15) | copy-start | bytes 61444
  156.2 17.3 %all-to-all-start.2 = ((bf16[128,4,1280]{0,2,1:T(8,128)(2,1)}), bf16[128,4,1280]{0,2,1:T(8,128)(2,1)S(1)}, u32[]{:S(2)}, u32[]{:S(2)}) async-start(bf16[128,4,1280]{0,2,1:T(8,128)(2,1)} %bitcast.12), calls=%async_computation.2 | async-start | bytes 2621440 | tf_op jit(solution)/shard_map/all_to_all | solution.py:122
  159.8 175.1 %all-reduce.8.cloned.1.call-start = ((), (), s32[]{:S(2)}) async-start(), calls=%async_computation.7 | async-start | bytes 163840 | tf_op jit(solution)/shard_map/psum | solution.py:201
  174.1 2.0 copy-start.3
  180.4 4.3 copy-start.2
  186.8 4.9 %copy-start.6 = (f32[512,20,64]{0,2,1:T(8,128)S(1)}, f32[512,20,64]{0,2,1:T(8,128)}, u32[]{:S(2)}) copy-start(f32[512,20,64]{0,2,1:T(8,128)} %reshape.166) | copy-start | bytes 7864324
  186.8 4.9 %copy-start.10 = (bf16[512,256]{1,0:T(8,128)(2,1)S(1)}, bf16[512,256]{1,0:T(8,128)(2,1)}, u32[]{:S(2)}) copy-start(bf16[512,256]{1,0:T(8,128)(2,1)} %copy-done.9) | copy-start | bytes 786436
  186.8 4.9 %copy-start.22 = (f32[20]{0:T(128)S(1)}, f32[20]{0:T(128)}, u32[]{:S(2)}) copy-start(f32[20]{0:T(128)} %param.24) | copy-start | bytes 244
  198.1 3.4 copy-start.4
  198.1 3.4 copy-start.19
  201.5 2.7 copy-start.17
  201.5 18.9 %copy-start.14 = (bf16[16,2560]{1,0:T(8,128)(2,1)S(1)}, bf16[16,2560]{1,0:T(8,128)(2,1)}, u32[]{:S(2)}) copy-start(bf16[16,2560]{1,0:T(8,128)(2,1)} %param.28) | copy-start | bytes 245764
  280.6 108.3 %all-reduce.6.cloned.1.call-start = ((), (), s32[]{:S(2)}) async-start(), calls=%async_computation.6 | async-start | bytes 163840 | tf_op jit(solution)/shard_map/psum | solution.py:200
  281.9 153.3 %reduce-scatter.2.cloned.1.call-start = ((), (), s32[]{:S(2)}) async-start(), calls=%async_computation.5 | async-start | bytes 3276800 | tf_op jit(solution)/shard_map/reduce_scatter | solution.py:175
  (2 other events, 1.3 us)
Sparse Core Ops, SparseCore 0:
  153.6 9.6 all-gather.6
  164.9 126.6 all-gather.4
  295.1 39.6 all-reduce.7
  337.6 51.2 all-reduce.5
  392.3 42.9 reduce-scatter.1
where the time goes:
time: 448 us; the launch traced here: 443 us
  waiting for transfers between devices  151 us (34%)
  local copies, waits for them, and re-layouts  105 us (23%)
  blocking collectives  96.8 us (22%)
  matrix products  41.7 us (9%)
  other arithmetic  17.6 us (4%)
  starting transfers between devices  16 us (4%)
  between operations  14.8 us (3%)
    dynamic_update_slice x4, local copies, waits for them, and re-layouts, ssd_blocks(): lax.scan(advance, start_state, (x_heads.reshape(blocks, block_len, head_c...  56.8 us
    psum x1, waiting for transfers between devices, shards(): lax.psum((grad_a_local, grad_b_local), ('context', 'fsdp'))  52.5 us
    psum x1, blocking collectives, shards(): lax.psum((grad_a_local, grad_b_local), ('context', 'fsdp'))  51.7 us
    reduce_scatter x1, waiting for transfers between devices, shards(): lax.psum_scatter((row_slice(scale_all, start_row, lax.axis_size('tensor')...  46.4 us
    psum x1, waiting for transfers between devices, shards(): lax.psum(grad_b_part.astype(jnp.bfloat16), 'tensor').astype(jnp.float32)  35.1 us
    all_gather x1, blocking collectives, shards(): lax.all_gather(convolved[:, inner_width:], 'tensor', axis=0, tiled=True)  19.2 us
    psum x1, blocking collectives, shards(): lax.psum(adapter_piece.astype(jnp.bfloat16), 'tensor').astype(jnp.float32)  15.3 us
    dot_general x2, matrix products, advance(): jnp.einsum('hij,jhp->ihp', decay_mat * gram_mat[None], x_scaled, precisio...  11.9 us
  transfers between devices with their start and end apart: 9, of which 5 were waited for; matrix products, arithmetic and copies ran while one was open for 13% of the time, Pallas kernels for 0%

commit v1 on v0

v1 whole, which is shorter than its diff:
```python
import functools
import math

import jax
import jax.numpy as jnp
from jax import lax
from jax.experimental import pallas as pl
from jax.experimental.pallas import tpu as pltpu
from jax.sharding import PartitionSpec as P

epsilon = 1e-05
LANES = 128
f32, bf16 = jnp.float32, jnp.bfloat16
HIGHEST = lax.Precision.HIGHEST


def exchange(value, axis):
    return lax.all_to_all(value, axis, split_axis=0, concat_axis=0, tiled=False)


def spread(value, axis, count):
    return exchange(jnp.broadcast_to(value[None], (count,) + value.shape), axis)


def silu(value):
    return 0.5 * value * (1.0 + jnp.tanh(0.5 * value))


def dot_nt(a, b, precision=None):
    return lax.dot_general(a, b, (((1,), (1,)), ((), ())), precision=precision, preferred_element_type=f32)


def dot_tn(a, b, precision=None):
    return lax.dot_general(a, b, (((0,), (0,)), ((), ())), precision=precision, preferred_element_type=f32)


def dot_nn(a, b, precision=None):
    return jnp.dot(a, b, precision=precision, preferred_element_type=f32)


def paired(table, pair, low_half, shape):
    first = jnp.broadcast_to(table[:, 2 * pair : 2 * pair + 1], shape)
    second = jnp.broadcast_to(table[:, 2 * pair + 1 : 2 * pair + 2], shape)
    return jnp.where(low_half, first, second)


def states_body(width, state, chunk, blocks, raw, rim, taps, bias, step_bias, rate, xconv, bc_out, step_out, cum_out, cumt_out, end_out, total_out, prev):
    joint = width + 2 * state
    prev[...] = rim[...].astype(f32)
    end_out[...] = jnp.zeros_like(end_out)
    total_out[...] = jnp.zeros_like(total_out)
    rows = lax.broadcasted_iota(jnp.int32, (chunk, chunk), 0)
    cols = lax.broadcasted_iota(jnp.int32, (chunk, chunk), 1)
    lower = (rows >= cols).astype(f32)
    low_half = lax.broadcasted_iota(jnp.int32, (chunk, LANES), 1) < LANES // 2
    low_row = lax.broadcasted_iota(jnp.int32, (1, LANES), 1) < LANES // 2
    count = taps.shape[0]

    def convolved(block, start):
        part = pl.ds(start, LANES)
        here = raw[block, :, part].astype(f32)
        cat = jnp.concatenate([prev[:, part], here], axis=0)
        total = bias[0:1, part] + taps[count - 1 : count, part] * here
        for k in range(count - 1):
            shift = 8 - (count - 1) + k
            total = total + taps[k : k + 1, part] * cat[shift : shift + chunk]
        prev[:, part] = here[chunk - 8 :]
        return silu(total).astype(bf16)

    def one(block, carry):
        log_steps = raw[block, :, joint : joint + LANES].astype(f32) + step_bias[...]
        step = jnp.maximum(log_steps, 0.0) + jnp.log1p(jnp.exp(-jnp.abs(log_steps)))
        decay = -step * rate[...]
        cum = dot_nn(lower, decay, HIGHEST)
        cumt = dot_tn(decay, (rows <= cols).astype(f32), HIGHEST)
        step_out[block] = step
        cum_out[block] = cum
        cumt_out[block] = cumt[: cumt_out.shape[1]]
        last = cum[chunk - 1 : chunk]
        tail = step * jnp.exp(last - cum)
        whole = jnp.exp(last)
        total_out[...] = total_out[...] + last
        for start in range(width, joint, LANES):
            bc_out[block, :, start - width : start - width + LANES] = convolved(block, start)
        b_t = bc_out[block, :, 0:state].T
        for pair in range(width // LANES):
            part = pl.ds(pair * LANES, LANES)
            x = convolved(block, pair * LANES)
            xconv[block, :, part] = x
            scaled = (x.astype(f32) * paired(tail, pair, low_half, (chunk, LANES))).astype(bf16)
            end_out[:, part] = paired(whole, pair, low_row, (1, LANES)) * end_out[:, part] + dot_nn(b_t, scaled)
        return carry

    lax.fori_loop(0, blocks, one, 0)


def outputs_body(width, state, chunk, blocks, xconv, bc, step_in, cum_in, cumt_in, start_state, gate, skip, gain, down_t, gated_out, stats, now):
    now[...] = start_state[...]
    rows = lax.broadcasted_iota(jnp.int32, (chunk, chunk), 0)
    cols = lax.broadcasted_iota(jnp.int32, (chunk, chunk), 1)
    causal = rows >= cols
    low_half = lax.broadcasted_iota(jnp.int32, (chunk, LANES), 1) < LANES // 2
    low_row = lax.broadcasted_iota(jnp.int32, (1, LANES), 1) < LANES // 2
    rank = down_t.shape[0]

    def one(block, carry):
        b_rows = bc[block, :, 0:state]
        c_rows = bc[block, :, state : 2 * state]
        b_t = b_rows.T
        gram = dot_nt(c_rows, b_rows)
        step = step_in[block]
        cum = cum_in[block]
        cumt = cumt_in[block]
        last = cum[chunk - 1 : chunk]
        reach = jnp.exp(cum)
        fade = jnp.exp(last - cum)
        whole = jnp.exp(last)
        squares = jnp.zeros((chunk, LANES), f32)
        for pair in range(width // LANES):
            part = pl.ds(pair * LANES, LANES)
            x = xconv[block, :, part].astype(f32)
            scaled = x * paired(step, pair, low_half, (chunk, LANES))
            mats = []
            for head in (2 * pair, 2 * pair + 1):
                gap = cum[:, head : head + 1] - cumt[head : head + 1, :]
                mats.append((jnp.exp(jnp.where(causal, gap, -jnp.inf)) * gram).astype(bf16))
            mat = jnp.concatenate(mats, axis=1)
            stacked = jnp.concatenate([jnp.where(low_half, scaled, 0.0), jnp.where(low_half, 0.0, scaled)], axis=0)
            y = dot_nn(mat, stacked.astype(bf16))
            old = now[:, part]
            y = y + paired(reach, pair, low_half, (chunk, LANES)) * dot_nn(c_rows, old.astype(bf16))
            faded = (scaled * paired(fade, pair, low_half, (chunk, LANES))).astype(bf16)
            now[:, part] = paired(whole, pair, low_row, (1, LANES)) * old + dot_nn(b_t, faded)
            y = y + skip[0:1, part] * x
            gated = y * silu(gate[block, :, part].astype(f32))
            squares = squares + gated * gated
            gated_out[block, :, part] = (gated * gain[0:1, part]).astype(bf16)
        stats[block, 0:rank] = dot_nt(down_t[...], gated_out[block])
        stats[block, rank : rank + 8] = dot_nt(jnp.ones((8, LANES), f32), squares, HIGHEST)
        return carry

    lax.fori_loop(0, blocks, one, 0)


def starting_state(state_end, total_row, heads):
    count = lax.axis_size("context")
    if count == 1:
        return jnp.zeros_like(state_end)
    if count == 2:
        return lax.ppermute(state_end, "context", [(0, 1)])
    mine = lax.axis_index("context")
    ends = lax.all_gather(state_end, "context")
    decays = lax.all_gather(total_row, "context")
    repeated = state_end.shape[1] // heads

    def lap(position, so_far):
        factor = jnp.repeat(jnp.exp(decays[position, :heads]), repeated)
        longer = factor[None, :] * so_far + ends[position]
        return jnp.where(position < mine, longer, so_far)

    return lax.fori_loop(0, count - 1, lap, jnp.zeros_like(state_end))


def shards(
    input_raw,
    state_proj_raw,
    gate_branch,
    step_raw,
    convolution_taps,
    convolution_bias,
    step_bias,
    decay_log_rate,
    skip_weight,
    gated_norm_gain,
    output_weight,
    adapter_down,
    adapter_up,
    cotangent,
):
    chunk = input_raw.shape[1]
    inner_width = input_raw.shape[2]
    state = state_proj_raw.shape[2] // 2
    taps = convolution_taps.shape[0]
    heads = step_bias.shape[0]
    width = gated_norm_gain.shape[0]
    head_size = width // heads
    model = cotangent.shape[2]
    rank = adapter_up.shape[0]
    tensor = lax.axis_size("tensor")
    context = lax.axis_size("context")
    fsdp = lax.axis_size("fsdp")
    mine = lax.axis_index("tensor")
    joint = width + 2 * state

    def by_group(values):
        return values.reshape(values.shape[0], tensor, -1).transpose(1, 0, 2)

    shared = jnp.broadcast_to(state_proj_raw, (tensor, chunk, 2 * state))
    steps = jnp.pad(by_group(step_raw[0]), ((0, 0), (0, 0), (0, LANES - heads)))
    raw = exchange(jnp.concatenate([by_group(input_raw[0]), shared, steps], axis=2), "tensor")
    edge = jnp.concatenate([by_group(input_raw[0, chunk - 8 :]), shared[:, chunk - 8 :]], axis=2)
    edges = jnp.broadcast_to(edge[None], (context,) + edge.shape).reshape((context * tensor,) + edge.shape[1:])
    edges = exchange(edges, ("context", "tensor"))
    place = lax.axis_index("context")
    rim = lax.dynamic_index_in_dim(edges, jnp.maximum(place * tensor - 1, 0), 0, keepdims=False)
    rim = jnp.where(place > 0, rim, jnp.zeros_like(rim))
    late = exchange(jnp.concatenate([by_group(gate_branch[0]), by_group(cotangent[0])], axis=2), "tensor")
    halves = 2 if context % 2 == 0 else 1
    half_rows = width // halves
    parity = place % halves
    own_half = lax.dynamic_slice_in_dim(output_weight, parity * half_rows, half_rows, 0)
    gathered = spread(own_half, "fsdp", fsdp)
    if halves == 2:
        other = lax.ppermute(gathered, "context", [(i, i ^ 1) for i in range(context)])
        gathered = jnp.concatenate([gathered, other], axis=1)
    columns = gathered.transpose(1, 0, 2).reshape(width, model)

    group = lambda values: lax.dynamic_slice_in_dim(values, mine * width, width, values.ndim - 1)
    taps_here = jnp.concatenate([group(convolution_taps), convolution_taps[:, inner_width:]], axis=1)
    bias_here = jnp.concatenate([group(convolution_bias), convolution_bias[inner_width:]])[None]
    row = lambda values: jnp.pad(values, (0, LANES - heads))[None]
    head_rows = -(-heads // 8) * 8
    vmem = pltpu.CompilerParams(vmem_limit_bytes=48 * 2**20)
    sds = jax.ShapeDtypeStruct
    xconv, bc, step, cum, cumt, state_end, total = pl.pallas_call(
        functools.partial(states_body, width, state, chunk, tensor),
        out_shape=(
            sds((tensor, chunk, width), bf16),
            sds((tensor, chunk, 2 * state), bf16),
            sds((tensor, chunk, LANES), f32),
            sds((tensor, chunk, LANES), f32),
            sds((tensor, head_rows, chunk), f32),
            sds((state, width), f32),
            sds((1, LANES), f32),
        ),
        scratch_shapes=[pltpu.VMEM((8, joint), f32)],
        compiler_params=vmem,
        name="span_states",
    )(raw, rim, taps_here, bias_here, row(step_bias), row(jnp.exp(decay_log_rate)))
    start_state = starting_state(state_end, total[0], heads)
    gated_out, stats = pl.pallas_call(
        functools.partial(outputs_body, width, state, chunk, tensor),
        out_shape=(sds((tensor, chunk, width), bf16), sds((tensor, rank + 8, chunk), f32)),
        scratch_shapes=[pltpu.VMEM((state, width), f32)],
        compiler_params=vmem,
        name="span_outputs",
    )(
        xconv, bc, step, cum, cumt, start_state, late[:, :, :width],
        jnp.repeat(skip_weight, head_size)[None], gated_norm_gain[None], adapter_down.T,
    )

    cot_rank = dot_nt(adapter_up, cotangent[0])
    packed = jnp.concatenate([stats.reshape(tensor * (rank + 8), chunk), cot_rank], axis=0)
    packed = spread(packed, "tensor", tensor)
    sums = jnp.sum(packed[:, : tensor * (rank + 8)], axis=0).reshape(tensor, rank + 8, chunk)
    scale = lax.rsqrt(sums[:, rank] / inner_width + epsilon)
    adapter = sums[:, :rank].astype(bf16)
    factor = 2.0 / math.sqrt(chunk * context * tensor * fsdp)
    weighted = (factor * scale[:, None, :] * adapter.astype(f32)).transpose(1, 0, 2).reshape(rank, -1)
    grad_rows = (factor * scale[:, None, :] * packed[:, tensor * (rank + 8) :]).transpose(1, 0, 2).reshape(rank, -1)

    span = tensor * chunk
    flat = gated_out.reshape(span, width)
    if halves == 2:
        ordered = jnp.concatenate(
            [lax.dynamic_slice_in_dim(flat, half * half_rows, half_rows, 1) for half in (parity, 1 - parity)], axis=1
        )
    else:
        ordered = flat
    frozen = dot_nn(ordered, columns).astype(bf16).reshape(tensor, chunk, model)
    pieces = exchange(frozen, "tensor")

    grad_b_part = dot_nn(weighted.astype(bf16), late[:, :, width:].reshape(span, -1))
    grad_a_part = dot_nn(grad_rows.astype(bf16), flat)
    both = spread(jnp.concatenate([grad_a_part, grad_b_part], axis=1), ("context", "fsdp"), context * fsdp)
    both = jnp.sum(both, axis=0)
    grad_a = both[:, :width].T
    grad_b = spread(both[:, width:], "tensor", tensor).transpose(1, 0, 2).reshape(rank, model)

    own_scale = lax.dynamic_index_in_dim(scale, mine, 0, keepdims=False)
    own_adapter = lax.dynamic_index_in_dim(adapter, mine, 0, keepdims=False)
    summed = jnp.sum(pieces.astype(f32), axis=0) + 2.0 * dot_tn(own_adapter, adapter_up)
    mixed = (own_scale[:, None] * summed).astype(bf16)
    return (mixed[None], grad_a, grad_b)


def solution(mesh):
    placed = (
        P("fsdp", ("context", "tensor"), None),
        P("fsdp", ("context", "tensor"), None),
        P("fsdp", ("context", "tensor"), None),
        P("fsdp", ("context", "tensor"), None),
        P(),
        P(),
        P("tensor"),
        P("tensor"),
        P("tensor"),
        P("tensor"),
        P("tensor", "fsdp"),
        P("tensor", None),
        P(),
        P("fsdp", ("context", "tensor"), None),
    )
    return jax.shard_map(
        shards,
        mesh=mesh,
        in_specs=placed,
        out_specs=(P("fsdp", ("context", "tensor"), None), P("tensor", None), P()),
        check_vma=False,
    )
```

time: 448 us -> 255 us (0.57)
  blocking collectives: 96.8 us -> 8.17 us
  local copies, waits for them, and re-layouts: 105 us -> 38.8 us
  matrix products: 41.7 us -> 9.12 us
  starting transfers between devices: 16 us -> 32.3 us
  waiting for transfers between devices: 151 us -> 137 us
  between operations: 14.8 us -> 0.93 us
  Pallas kernels: 0 us -> 13.7 us
    all_to_all x3 -> x7, waiting for transfers between devices: 6.92 us -> 137 us  [exchange(): return lax.all_to_all(value, axis, split_axis=0, concat_axis=0, tiled=False)]
    psum x2 -> x0, waiting for transfers between devices: 87.6 us -> none  [the longest x1 52.5 us: shards(): lax.psum((grad_a_local, grad_b_local), ('context', 'fsdp'))]
    psum x2 -> x0, blocking collectives: 67 us -> none  [the longest x1 51.7 us: shards(): lax.psum((grad_a_local, grad_b_local), ('context', 'fsdp'))]
    dynamic_update_slice x4 -> x0, local copies, waits for them, and re-layouts: 56.8 us -> none  [ssd_blocks(): lax.scan(advance, start_state, (x_heads.reshape(blocks, block_len, head_c...]
    reduce_scatter x1 -> x0, waiting for transfers between devices: 46.4 us -> none  [shards(): lax.psum_scatter((row_slice(scale_all, start_row, lax.axis_size('tensor')...]
    dot_general x15 -> x5, matrix products: 41.7 us -> 9.12 us  [the longest x3 6.53 us: dot_nn(): return jnp.dot(a, b, precision=precision, preferred_element_type=f32)]
    all_gather x2 -> x0, blocking collectives: 27.3 us -> none  [the longest x1 19.2 us: shards(): lax.all_gather(convolved[:, inner_width:], 'tensor', axis=0, tiled=True)]
    all_to_all x3 -> x7, starting transfers between devices: 11 us -> 30.8 us  [exchange(): return lax.all_to_all(value, axis, split_axis=0, concat_axis=0, tiled=False)]
  transfers between devices with their start and end apart: 9 -> 9, of which waited for: 5 -> 5; matrix products, arithmetic and copies ran while one was open for 13% -> 18% of each run, Pallas kernels for 0% -> 5%
where the time goes in v1:
time: 255 us; the launch traced here: 254 us
  waiting for transfers between devices  137 us (54%)
  local copies, waits for them, and re-layouts  38.8 us (15%)
  starting transfers between devices  32.3 us (13%)
  Pallas kernels  13.7 us (5%)
  other arithmetic  13.5 us (5%)
  matrix products  9.12 us (4%)
  blocking collectives  8.17 us (3%)
    all_to_all x7, waiting for transfers between devices, exchange(): return lax.all_to_all(value, axis, split_axis=0, concat_axis=0, tiled=False)  137 us
    all_to_all x7, starting transfers between devices, exchange(): return lax.all_to_all(value, axis, split_axis=0, concat_axis=0, tiled=False)  30.8 us
    unnamed x39, local copies, waits for them, and re-layouts  12.4 us
    pallas_call x1, Pallas kernels, shards(): pl.pallas_call(functools.partial(outputs_body, width, state, chunk, tenso...  8.34 us
    all_to_all x1, blocking collectives, exchange(): return lax.all_to_all(value, axis, split_axis=0, concat_axis=0, tiled=False)  8.17 us
    dot_general x3, matrix products, dot_nn(): return jnp.dot(a, b, precision=precision, preferred_element_type=f32)  6.53 us
    another operation x5, local copies, waits for them, and re-layouts, by_group(): return values.reshape(values.shape[0], tensor, -1).transpose(1, 0, 2)  6.23 us
    pallas_call x1, Pallas kernels, shards(): pl.pallas_call(functools.partial(states_body, width, state, chunk, tensor...  5.38 us
  transfers between devices with their start and end apart: 9, of which 5 were waited for; matrix products, arithmetic and copies ran while one was open for 18% of the time, Pallas kernels for 5%

profile of v1, /device:TPU:0, one launch (start us, length us, event | category | flops | bytes accessed | tf_op | source)
XLA Modules:
  0.0 253.5 jit_solution(4462904654829318335)
XLA Ops:
  3.1 5.2 %all-to-all-start.1 = ((bf16[8,8,1536]{2,1,0:T(8,128)(2,1)}), bf16[8,8,1536]{2,1,0:T(8,128)(2,1)S(1)}, u32[]{:S(2)}, u32[]{:S(2)}) async-start(bf16[8,8,1536]{2,1,0:T(8,128)(2,1)} %bitcast.7), calls=%async_computation.1 | async-start | bytes 393216 | tf_op jit(solution)/shard_map/all_to_all | solution.py:18
  8.3 1.8 copy.42
  10.2 1.4 copy.43
  11.7 2.7 %fusion.5 = bf16[4,128,1664]{2,1,0:T(8,128)(2,1)} fusion(bf16[4,128,20]{2,1,0:T(8,128)(2,1)S(1)} %bitcast.72, bf16[4,128,256]{2,1,0:T(8,128)(2,1)S(1)} %broadcast_in_dim.31, bf16[4,128,1280]{2,1,0:T(8,128)(2,1)} %bitcast.65), kind=kLoop, calls=%fused_computation.12 | loop fusion | flops 6815744 | bytes 3297280 | tf_op jit(solution)/shard_map/concatenate | solution.py:200
  14.4 4.2 %all-to-all-start = ((bf16[4,128,1664]{2,1,0:T(8,128)(2,1)}), bf16[4,128,1664]{2,1,0:T(8,128)(2,1)S(1)}, u32[]{:S(2)}, u32[]{:S(2)}) async-start(bf16[4,128,1664]{2,1,0:T(8,128)(2,1)} %fusion.5), calls=%async_computation | async-start | bytes 3407872 | tf_op jit(solution)/shard_map/all_to_all | solution.py:18
  19.6 2.2 copy.49
  21.7 17.8 %all-to-all-done.raw = bf16[4,128,1664]{2,1,0:T(8,128)(2,1)S(1)} async-done(((bf16[4,128,1664]{2,1,0:T(8,128)(2,1)}), bf16[4,128,1664]{2,1,0:T(8,128)(2,1)S(1)}, u32[]{:S(2)}, u32[]{:S(2)}) %all-to-all-start) | async-done | bytes 1703968 | tf_op jit(solution)/shard_map/all_to_all | solution.py:18
  39.5 3.1 %broadcast_in_dim.74 = bf16[4,640,640]{1,2,0:T(8,128)(2,1)} broadcast(bf16[640,640]{0,1:T(8,128)(2,1)} %copy.49), dimensions={1,2} | broadcast | bytes 4096000 | tf_op jit(solution)/shard_map/broadcast_in_dim | solution.py:22
  42.7 4.9 %all-to-all-start.4 = ((bf16[4,640,640]{1,2,0:T(8,128)(2,1)}), bf16[4,640,640]{1,2,0:T(8,128)(2,1)}, u32[]{:S(2)}, u32[]{:S(2)}) async-start(bf16[4,640,640]{1,2,0:T(8,128)(2,1)} %broadcast_in_dim.74), calls=%async_computation.4 | async-start | bytes 6553600 | tf_op jit(solution)/shard_map/all_to_all | solution.py:18
  49.6 2.2 copy.47
  51.7 2.2 copy.48
  53.9 2.5 copy.45
  56.4 2.4 copy.46
  58.8 3.0 %pad_maximum_fusion.1 = bf16[4,128,1920]{2,1,0:T(8,128)(2,1)} fusion(bf16[4,128,640]{2,1,0:T(8,128)(2,1)} %bitcast.70, bf16[4,128,1280]{2,1,0:T(8,128)(2,1)} %bitcast.67), kind=kLoop, calls=%fused_computation.11 | loop fusion | flops 3932160 | bytes 3932160 | tf_op jit(solution)/shard_map/concatenate | solution.py:207
  61.9 58.5 %all-to-all-done.4 = bf16[4,640,640]{1,2,0:T(8,128)(2,1)} async-done(((bf16[4,640,640]{1,2,0:T(8,128)(2,1)}), bf16[4,640,640]{1,2,0:T(8,128)(2,1)}, u32[]{:S(2)}, u32[]{:S(2)}) %all-to-all-start.4) | async-done | bytes 3276832 | tf_op jit(solution)/shard_map/all_to_all | solution.py:18
  120.4 4.4 %all-to-all-start.2 = ((bf16[4,128,1920]{2,1,0:T(8,128)(2,1)}), bf16[4,128,1920]{2,1,0:T(8,128)(2,1)}, u32[]{:S(2)}, u32[]{:S(2)}) async-start(bf16[4,128,1920]{2,1,0:T(8,128)(2,1)} %pad_maximum_fusion.1), calls=%async_computation.2 | async-start | bytes 3932160 | tf_op jit(solution)/shard_map/all_to_all | solution.py:18
  128.3 5.4 %span_states.1 = (bf16[4,128,1280]{2,1,0:T(8,128)(2,1)S(1)}, bf16[4,128,256]{2,1,0:T(8,128)(2,1)S(1)}, f32[4,128,128]{2,1,0:T(8,128)S(1)}, f32[4,128,128]{2,1,0:...) custom-call(bf16[4,128,1664]{2,1,0:T(8,128)(2,1)S(1)} %all-to-all-done.raw, ...), custom_call_target="tpu_custom_call" | custom-call | tf_op jit(solution)/shard_map/span_states/pallas_call | solution.py:225
  136.9 1.4 collective-permute-start
  139.2 1.4 fusion.10
  140.6 7.2 %all-to-all-done.2 = bf16[4,128,1920]{2,1,0:T(8,128)(2,1)} async-done(((bf16[4,128,1920]{2,1,0:T(8,128)(2,1)}), bf16[4,128,1920]{2,1,0:T(8,128)(2,1)}, u32[]{:S(2)}, u32[]{:S(2)}) %all-to-all-start.2) | async-done | bytes 1966112 | tf_op jit(solution)/shard_map/all_to_all | solution.py:18
  147.9 1.5 slice.54.gate
  152.1 8.3 %span_outputs.1 = (bf16[4,128,1280]{2,1,0:T(8,128)(2,1)S(1)}, f32[4,24,128]{2,1,0:T(8,128)S(1)}) custom-call(bf16[4,128,1280]{2,1,0:T(8,128)(2,1)S(1)} %copy-done.2, bf16[4,128,256]{2,1,0:T(8,128)(2,1)S(1)} %copy-done.6, f32[4,128,128]{2,1,0:T(8,128)S(1)} %copy-done.8, f32[4,128,128]{2,1,0:T(8,128)S(1)} %copy-done.10, ...), custom_call_target="tpu_custom_call" | custom-call | tf_op jit(solution)/shard_map/span_outputs/pallas_call | solution.py:241
  160.5 8.2 %all_to_all.40 = f32[4,112,128]{2,1,0:T(8,128)S(1)} all-to-all(f32[4,112,128]{2,1,0:T(8,128)S(1)} %broadcast_in_dim.73), channel_id=1, replica_groups=mesh['context'=2,'tensor'=4,'fsdp'=4] {'tensor'}, dimensions={0} | all-to-all | bytes 458752 | tf_op jit(solution)/shard_map/all_to_all | solution.py:18
  168.7 1.3 convolution_bitcast_fusion.1
  171.4 4.2 %all-to-all-start.6 = ((f32[8,16,1920]{2,1,0:T(8,128)}), f32[8,16,1920]{2,1,0:T(8,128)}, u32[]{:S(2)}, u32[]{:S(2)}) async-start(f32[8,16,1920]{2,1,0:T(8,128)} %broadcast_in_dim.76), calls=%async_computation.6 | async-start | bytes 1966080 | tf_op jit(solution)/shard_map/all_to_all | solution.py:18
  176.9 23.4 %all-to-all-done.6 = f32[8,16,1920]{2,1,0:T(8,128)} async-done(((f32[8,16,1920]{2,1,0:T(8,128)}), f32[8,16,1920]{2,1,0:T(8,128)}, u32[]{:S(2)}, u32[]{:S(2)}) %all-to-all-start.6) | async-done | bytes 983072 | tf_op jit(solution)/shard_map/all_to_all | solution.py:18
  202.2 3.3 %all-to-all-start.7 = ((f32[4,16,640]{2,1,0:T(8,128)}), f32[4,16,640]{2,1,0:T(8,128)S(1)}, u32[]{:S(2)}, u32[]{:S(2)}) async-start(f32[4,16,640]{2,1,0:T(8,128)} %broadcast_in_dim.77), calls=%async_computation.7 | async-start | bytes 327680 | tf_op jit(solution)/shard_map/all_to_all | solution.py:18
  205.6 3.5 %pad_maximum_fusion = bf16[4,1280,640]{1,2,0:T(8,128)(2,1)S(1)} fusion(bf16[4,640,640]{1,2,0:T(8,128)(2,1)} %collective-permute-done.1, bf16[4,640,640]{1,2,0:T(8,128)(2,1)} %all-to-all-done.4), kind=kLoop, calls=%fused_computation | loop fusion | flops 13107200 | bytes 13107200 | tf_op jit(solution)/shard_map/concatenate | solution.py:215
  209.1 5.0 %convolution_convert_fusion = bf16[512,2560]{1,0:T(8,128)(2,1)} fusion(bf16[1280,2560]{0,1:T(8,128)(2,1)S(1)} %bitcast.63, bf16[512,640]{1,0:T(8,128)(2,1)S(1)} %copy-done.13, bf16[512,640]{1,0:T(8,128)(2,1)S(1)} %copy-done.12), kind=kOutput, calls=%fused_computation.2 | convolution fusion | flops 3359375360 | bytes 10485760 | tf_op jit(solution)/shard_map/dot_general | solution.py:38
  214.1 4.5 %all-to-all-start.5 = ((bf16[4,128,2560]{2,1,0:T(8,128)(2,1)}), bf16[4,128,2560]{2,1,0:T(8,128)(2,1)}, u32[]{:S(2)}, u32[]{:S(2)}) async-start(bf16[4,128,2560]{2,1,0:T(8,128)(2,1)} %bitcast.68), calls=%async_computation.5 | async-start | bytes 5242880 | tf_op jit(solution)/shard_map/all_to_all | solution.py:18
  220.0 30.0 %all-to-all-done.5 = bf16[4,128,2560]{2,1,0:T(8,128)(2,1)} async-done(((bf16[4,128,2560]{2,1,0:T(8,128)(2,1)}), bf16[4,128,2560]{2,1,0:T(8,128)(2,1)}, u32[]{:S(2)}, u32[]{:S(2)}) %all-to-all-start.5) | async-done | bytes 2621472 | tf_op jit(solution)/shard_map/all_to_all | solution.py:18
  250.0 2.3 convert_reduce_fusion
  (79 shorter events, 23.1 us)
Async XLA Ops:
  0.6 18.0 %copy-start = (bf16[1280,640]{1,0:T(8,128)(2,1)S(1)}, bf16[1280,640]{1,0:T(8,128)(2,1)}, u32[]{:S(2)}) copy-start(bf16[1280,640]{1,0:T(8,128)(2,1)} %param.24) | copy-start | bytes 4915204
  0.6 9.4 %copy-start.16 = (bf16[1,128,80]{1,2,0:T(8,128)(2,1)S(1)}, bf16[1,128,80]{1,2,0:T(8,128)(2,1)}, u32[]{:S(2)}) copy-start(bf16[1,128,80]{1,2,0:T(8,128)(2,1)} %param.17) | copy-start | bytes 61444
  3.1 11.3 %all-to-all-start.1 = ((bf16[8,8,1536]{2,1,0:T(8,128)(2,1)}), bf16[8,8,1536]{2,1,0:T(8,128)(2,1)S(1)}, u32[]{:S(2)}, u32[]{:S(2)}) async-start(bf16[8,8,1536]{2,1,0:T(8,128)(2,1)} %bitcast.7), calls=%async_computation.1 | async-start | bytes 393216 | tf_op jit(solution)/shard_map/all_to_all | solution.py:18
  10.0 1.6 copy-start.15
  14.4 25.2 %all-to-all-start = ((bf16[4,128,1664]{2,1,0:T(8,128)(2,1)}), bf16[4,128,1664]{2,1,0:T(8,128)(2,1)S(1)}, u32[]{:S(2)}, u32[]{:S(2)}) async-start(bf16[4,128,1664]{2,1,0:T(8,128)(2,1)} %fusion.5), calls=%async_computation | async-start | bytes 3407872 | tf_op jit(solution)/shard_map/all_to_all | solution.py:18
  42.7 77.7 %all-to-all-start.4 = ((bf16[4,640,640]{1,2,0:T(8,128)(2,1)}), bf16[4,640,640]{1,2,0:T(8,128)(2,1)}, u32[]{:S(2)}, u32[]{:S(2)}) async-start(bf16[4,640,640]{1,2,0:T(8,128)(2,1)} %broadcast_in_dim.74), calls=%async_computation.4 | async-start | bytes 6553600 | tf_op jit(solution)/shard_map/all_to_all | solution.py:18
  120.4 27.4 %all-to-all-start.2 = ((bf16[4,128,1920]{2,1,0:T(8,128)(2,1)}), bf16[4,128,1920]{2,1,0:T(8,128)(2,1)}, u32[]{:S(2)}, u32[]{:S(2)}) async-start(bf16[4,128,1920]{2,1,0:T(8,128)(2,1)} %pad_maximum_fusion.1), calls=%async_computation.2 | async-start | bytes 3932160 | tf_op jit(solution)/shard_map/all_to_all | solution.py:18
  125.5 13.7 %copy-start.17 = (f32[1280]{0:T(1024)S(1)}, f32[1280]{0:T(1024)}, u32[]{:S(2)}) copy-start(f32[1280]{0:T(1024)} %param.23) | copy-start | bytes 15364
  133.7 1.1 copy-start.1
  134.7 0.7 copy-start.5
  135.5 0.7 copy-start.7
  136.2 0.7 copy-start.9
  136.9 13.3 %copy-start.6 = (bf16[4,128,256]{2,1,0:T(8,128)(2,1)S(1)}, bf16[4,128,256]{2,1,0:T(8,128)(2,1)}, u32[]{:S(2)}) copy-start(bf16[4,128,256]{2,1,0:T(8,128)(2,1)} %copy-done.5) | copy-start | bytes 786436
  136.9 13.3 %copy-start.8 = (f32[4,128,128]{2,1,0:T(8,128)S(1)}, f32[4,128,128]{2,1,0:T(8,128)}, u32[]{:S(2)}) copy-start(f32[4,128,128]{2,1,0:T(8,128)} %copy-done.7) | copy-start | bytes 786436
  136.9 12.5 %collective-permute-start = (f32[128,1280]{1,0:T(8,128)}, f32[128,1280]{1,0:T(8,128)S(1)}, u32[]{:S(2)}, u32[]{:S(2)}) collective-permute-start(f32[128,1280]{1,0:T(8,128)} %get-tuple-element.16), channel_id=1, source_target_pairs={{0,16},{1,17},{2,18},{3,19},{4,20},{5,21},{6,22},{7,23},{8,24},{9,... | collective-permute-start | bytes 1966088 | tf_op jit(solution)/shard_map/ppermute | solution.py:150
  138.3 67.3 %collective-permute-start.1 = (bf16[4,640,640]{1,2,0:T(8,128)(2,1)}, bf16[4,640,640]{1,2,0:T(8,128)(2,1)}, u32[]{:S(2)}, u32[]{:S(2)}) collective-permute-start(bf16[4,640,640]{1,2,0:T(8,128)(2,1)} %all-to-all-done.4), channel_id=1, source_target_pairs={{0,16},{16,0},{1,17},{17,1},{2,18},{18,2},{3,19},{19,3},{4,20},{20... | collective-permute-start | bytes 9830408 | tf_op jit(solution)/shard_map/ppermute | solution.py:214
  147.8 2.4 copy-start.2
  147.8 2.4 copy-start.10
  149.4 0.8 copy-start.3
  150.2 1.1 copy-start.4
  151.3 0.8 copy-start.11
  171.4 28.9 %all-to-all-start.6 = ((f32[8,16,1920]{2,1,0:T(8,128)}), f32[8,16,1920]{2,1,0:T(8,128)}, u32[]{:S(2)}, u32[]{:S(2)}) async-start(f32[8,16,1920]{2,1,0:T(8,128)} %broadcast_in_dim.76), calls=%async_computation.6 | async-start | bytes 1966080 | tf_op jit(solution)/shard_map/all_to_all | solution.py:18
  202.2 11.9 %all-to-all-start.7 = ((f32[4,16,640]{2,1,0:T(8,128)}), f32[4,16,640]{2,1,0:T(8,128)S(1)}, u32[]{:S(2)}, u32[]{:S(2)}) async-start(f32[4,16,640]{2,1,0:T(8,128)} %broadcast_in_dim.77), calls=%async_computation.7 | async-start | bytes 327680 | tf_op jit(solution)/shard_map/all_to_all | solution.py:18
  205.6 3.5 %copy-start.12 = (bf16[512,640]{1,0:T(8,128)(2,1)S(1)}, bf16[512,640]{1,0:T(8,128)(2,1)}, u32[]{:S(2)}) copy-start(bf16[512,640]{1,0:T(8,128)(2,1)} %get-tuple-element.21) | copy-start | bytes 1966084
  205.6 3.5 %copy-start.13 = (bf16[512,640]{1,0:T(8,128)(2,1)S(1)}, bf16[512,640]{1,0:T(8,128)(2,1)}, u32[]{:S(2)}) copy-start(bf16[512,640]{1,0:T(8,128)(2,1)} %get-tuple-element.22) | copy-start | bytes 1966084
  214.1 35.9 %all-to-all-start.5 = ((bf16[4,128,2560]{2,1,0:T(8,128)(2,1)}), bf16[4,128,2560]{2,1,0:T(8,128)(2,1)}, u32[]{:S(2)}, u32[]{:S(2)}) async-start(bf16[4,128,2560]{2,1,0:T(8,128)(2,1)} %bitcast.68), calls=%async_computation.5 | async-start | bytes 5242880 | tf_op jit(solution)/shard_map/all_to_all | solution.py:18
  220.0 32.3 %copy-start.14 = (bf16[16,2560]{1,0:T(8,128)(2,1)S(1)}, bf16[16,2560]{1,0:T(8,128)(2,1)}, u32[]{:S(2)}) copy-start(bf16[16,2560]{1,0:T(8,128)(2,1)} %param.26) | copy-start | bytes 245764

commit v2 on v1

--- a/solution.py
+++ b/solution.py
@@ -8,6 +8,7 @@
 from jax.experimental.pallas import tpu as pltpu
 from jax.sharding import PartitionSpec as P
 
+
 epsilon = 1e-05
 LANES = 128
 f32, bf16 = jnp.float32, jnp.bfloat16
@@ -20,6 +21,54 @@
 
 def spread(value, axis, count):
     return exchange(jnp.broadcast_to(value[None], (count,) + value.shape), axis)
+
+
+def partner(index, step, count):
+    return index ^ step if count & (count - 1) == 0 else (index + step) % count
+
+
+def sender(index, step, count):
+    return index ^ step if count & (count - 1) == 0 else (index - step) % count
+
+
+def hop(value, axis, step, count):
+    return lax.ppermute(value, axis, [(i, partner(i, step, count)) for i in range(count)])
+
+
+def after(values, earlier):
+    return lax.optimization_barrier((values, earlier))[0]
+
+
+def along(value, axis, step):
+    count = lax.axis_size(axis)
+    return lax.ppermute(value, axis, [(i, i + step) for i in range(count) if 0 <= i + step < count])
+
+
+def pack_body(group_sizes, shared_sizes, *refs):
+    out = refs[-1]
+    parts = refs[: len(group_sizes)]
+    shared = refs[len(group_sizes) : -1]
+    order = [(parts[0], group_sizes[0], True)]
+    order += [(ref, size, False) for ref, size in zip(shared, shared_sizes)]
+    order += [(ref, size, True) for ref, size in zip(parts[1:], group_sizes[1:])]
+    for peer in range(out.shape[0]):
+        start = 0
+        for ref, size, split in order:
+            piece = ref[:, peer * size : (peer + 1) * size] if split else ref[...]
+            out[peer, :, start : start + size] = piece
+            start += size
+        if start < out.shape[2]:
+            out[peer, :, start:] = jnp.zeros((out.shape[1], out.shape[2] - start), out.dtype)
+
+
+def packed_for(peers, grouped, shared):
+    sizes = [part.shape[1] // peers for part in grouped]
+    shared_sizes = [part.shape[1] for part in shared]
+    total = -(-(sum(sizes) + sum(shared_sizes)) // LANES) * LANES
+    return pl.pallas_call(
+        functools.partial(pack_body, sizes, shared_sizes),
+        out_shape=jax.ShapeDtypeStruct((peers, grouped[0].shape[0], total), grouped[0].dtype),
+    )(*grouped, *shared)
 
 
 def silu(value):
@@ -94,14 +143,13 @@
     lax.fori_loop(0, blocks, one, 0)
 
 
-def outputs_body(width, state, chunk, blocks, xconv, bc, step_in, cum_in, cumt_in, start_state, gate, skip, gain, down_t, gated_out, stats, now):
+def recurrence_body(width, state, chunk, blocks, xconv, bc, step_in, cum_in, cumt_in, start_state, skip, y_out, now):
     now[...] = start_state[...]
     rows = lax.broadcasted_iota(jnp.int32, (chunk, chunk), 0)
     cols = lax.broadcasted_iota(jnp.int32, (chunk, chunk), 1)
     causal = rows >= cols
     low_half = lax.broadcasted_iota(jnp.int32, (chunk, LANES), 1) < LANES // 2
     low_row = lax.broadcasted_iota(jnp.int32, (1, LANES), 1) < LANES // 2
-    rank = down_t.shape[0]
 
     def one(block, carry):
         b_rows = bc[block, :, 0:state]
@@ -115,7 +163,6 @@
         reach = jnp.exp(cum)
         fade = jnp.exp(last - cum)
         whole = jnp.exp(last)
-        squares = jnp.zeros((chunk, LANES), f32)
         for pair in range(width // LANES):
             part = pl.ds(pair * LANES, LANES)
             x = xconv[block, :, part].astype(f32)
@@ -131,8 +178,20 @@
             y = y + paired(reach, pair, low_half, (chunk, LANES)) * dot_nn(c_rows, old.astype(bf16))
             faded = (scaled * paired(fade, pair, low_half, (chunk, LANES))).astype(bf16)
             now[:, part] = paired(whole, pair, low_row, (1, LANES)) * old + dot_nn(b_t, faded)
-            y = y + skip[0:1, part] * x
-            gated = y * silu(gate[block, :, part].astype(f32))
+            y_out[block, :, part] = y + skip[0:1, part] * x
+        return carry
+
+    lax.fori_loop(0, blocks, one, 0)
+
+
+def gating_body(width, chunk, blocks, y_in, gate, gain, down_t, gated_out, stats):
+    rank = down_t.shape[0]
+
+    def one(block, carry):
+        squares = jnp.zeros((chunk, LANES), f32)
+        for start in range(0, width, LANES):
+            part = pl.ds(start, LANES)
+            gated = y_in[block, :, part] * silu(gate[block, :, part].astype(f32))
             squares = squares + gated * gated
             gated_out[block, :, part] = (gated * gain[0:1, part]).astype(bf16)
         stats[block, 0:rank] = dot_nt(down_t[...], gated_out[block])
@@ -140,6 +199,19 @@
         return carry
 
     lax.fori_loop(0, blocks, one, 0)
+
+
+def mixed_body(fsdp, tensor, held, spot, scale, adapter, up, *refs):
+    out = refs[-1]
+    shard = out.shape[1] // fsdp
+    for turn, ks in enumerate(held):
+        for position, k in enumerate(ks):
+            total = 0.0
+            for ref in refs[turn * tensor : (turn + 1) * tensor]:
+                total = total + ref[:, position * shard : (position + 1) * shard].astype(f32)
+            place = pl.ds(pl.multiple_of(lax.rem(spot[0] + k, fsdp) * shard, LANES), shard)
+            total = total + 2.0 * dot_tn(adapter[...], up[:, place])
+            out[:, place] = (scale[...] * total).astype(bf16)
 
 
 def starting_state(state_end, total_row, heads):
@@ -180,7 +252,6 @@
     chunk = input_raw.shape[1]
     inner_width = input_raw.shape[2]
     state = state_proj_raw.shape[2] // 2
-    taps = convolution_taps.shape[0]
     heads = step_bias.shape[0]
     width = gated_norm_gain.shape[0]
     head_size = width // heads
@@ -192,28 +263,24 @@
     mine = lax.axis_index("tensor")
     joint = width + 2 * state
 
-    def by_group(values):
-        return values.reshape(values.shape[0], tensor, -1).transpose(1, 0, 2)
-
-    shared = jnp.broadcast_to(state_proj_raw, (tensor, chunk, 2 * state))
-    steps = jnp.pad(by_group(step_raw[0]), ((0, 0), (0, 0), (0, LANES - heads)))
-    raw = exchange(jnp.concatenate([by_group(input_raw[0]), shared, steps], axis=2), "tensor")
-    edge = jnp.concatenate([by_group(input_raw[0, chunk - 8 :]), shared[:, chunk - 8 :]], axis=2)
-    edges = jnp.broadcast_to(edge[None], (context,) + edge.shape).reshape((context * tensor,) + edge.shape[1:])
-    edges = exchange(edges, ("context", "tensor"))
+    def pieces_of(product):
+        return [lax.dynamic_index_in_dim(product, partner(mine, k, tensor), 0, keepdims=False) for k in range(tensor)]
+
+    def over_groups(pieces):
+        return [pieces[0]] + [hop(pieces[k], "tensor", k, tensor) for k in reversed(range(1, tensor))]
+
+    raw = exchange(packed_for(tensor, [input_raw[0], step_raw[0]], [state_proj_raw[0]]), "tensor")
+    rim = along(raw[tensor - 1, chunk - 8 :, :joint], "context", 1)
     place = lax.axis_index("context")
-    rim = lax.dynamic_index_in_dim(edges, jnp.maximum(place * tensor - 1, 0), 0, keepdims=False)
-    rim = jnp.where(place > 0, rim, jnp.zeros_like(rim))
-    late = exchange(jnp.concatenate([by_group(gate_branch[0]), by_group(cotangent[0])], axis=2), "tensor")
+    packed_gate = packed_for(tensor, [gate_branch[0]], [])
+    gate = exchange(packed_gate, "tensor")
     halves = 2 if context % 2 == 0 else 1
     half_rows = width // halves
     parity = place % halves
     own_half = lax.dynamic_slice_in_dim(output_weight, parity * half_rows, half_rows, 0)
-    gathered = spread(own_half, "fsdp", fsdp)
-    if halves == 2:
-        other = lax.ppermute(gathered, "context", [(i, i ^ 1) for i in range(context)])
-        gathered = jnp.concatenate([gathered, other], axis=1)
-    columns = gathered.transpose(1, 0, 2).reshape(width, model)
+    rising, falling = [own_half], [own_half]
+    rising.append(along(own_half, "fsdp", 1))
+    falling.append(along(own_half, "fsdp", -1))
 
     group = lambda values: lax.dynamic_slice_in_dim(values, mine * width, width, values.ndim - 1)
     taps_here = jnp.concatenate([group(convolution_taps), convolution_taps[:, inner_width:]], axis=1)
@@ -238,27 +305,45 @@
         name="span_states",
     )(raw, rim, taps_here, bias_here, row(step_bias), row(jnp.exp(decay_log_rate)))
     start_state = starting_state(state_end, total[0], heads)
-    gated_out, stats = pl.pallas_call(
-        functools.partial(outputs_body, width, state, chunk, tensor),
-        out_shape=(sds((tensor, chunk, width), bf16), sds((tensor, rank + 8, chunk), f32)),
+    y = pl.pallas_call(
+        functools.partial(recurrence_body, width, state, chunk, tensor),
+        out_shape=sds((tensor, chunk, width), f32),
         scratch_shapes=[pltpu.VMEM((state, width), f32)],
         compiler_params=vmem,
-        name="span_outputs",
-    )(
-        xconv, bc, step, cum, cumt, start_state, late[:, :, :width],
-        jnp.repeat(skip_weight, head_size)[None], gated_norm_gain[None], adapter_down.T,
-    )
+        name="span_recurrence",
+    )(xconv, bc, step, cum, cumt, start_state, jnp.repeat(skip_weight, head_size)[None])
+    packed_turn = after(packed_for(tensor, [cotangent[0]], []), y)
+    turned = exchange(packed_turn, "tensor")
+    waits = {1: raw, 2: y}
+    for step_index in range(1, fsdp - 1):
+        last_two = (rising[-1], falling[-1])
+        if step_index in waits:
+            last_two = after(last_two, waits[step_index])
+        rising.append(along(last_two[0], "fsdp", 1))
+        falling.append(along(last_two[1], "fsdp", -1))
+    ranked = sorted(range(fsdp), key=lambda k: (max(k, fsdp - k) if k else 0, k))
+    early, rest = ranked[: max(1, fsdp // 2)], ranked[max(1, fsdp // 2) :]
+
+    def assembled(ks, ends):
+        held = [own_half if k == 0 else ends[1][k] + ends[0][fsdp - k] for k in ks]
+        here = jnp.concatenate(held, axis=1)
+        if halves == 1:
+            return here
+        other = lax.ppermute(here, "context", [(i, i ^ 1) for i in range(context)])
+        return jnp.concatenate([here, other], axis=0)
+
+    gated_out, stats = pl.pallas_call(
+        functools.partial(gating_body, width, chunk, tensor),
+        out_shape=(sds((tensor, chunk, width), bf16), sds((tensor, rank + 8, chunk), f32)),
+        compiler_params=vmem,
+        name="span_gating",
+    )(y, gate, gated_norm_gain[None], adapter_down.T)
 
     cot_rank = dot_nt(adapter_up, cotangent[0])
     packed = jnp.concatenate([stats.reshape(tensor * (rank + 8), chunk), cot_rank], axis=0)
-    packed = spread(packed, "tensor", tensor)
-    sums = jnp.sum(packed[:, : tensor * (rank + 8)], axis=0).reshape(tensor, rank + 8, chunk)
-    scale = lax.rsqrt(sums[:, rank] / inner_width + epsilon)
-    adapter = sums[:, :rank].astype(bf16)
-    factor = 2.0 / math.sqrt(chunk * context * tensor * fsdp)
-    weighted = (factor * scale[:, None, :] * adapter.astype(f32)).transpose(1, 0, 2).reshape(rank, -1)
-    grad_rows = (factor * scale[:, None, :] * packed[:, tensor * (rank + 8) :]).transpose(1, 0, 2).reshape(rank, -1)
-
+    arrived = {0: packed}
+    for k in range(1, tensor):
+        arrived[k] = hop(packed, "tensor", k, tensor)
     span = tensor * chunk
     flat = gated_out.reshape(span, width)
     if halves == 2:
@@ -267,20 +352,48 @@
         )
     else:
         ordered = flat
-    frozen = dot_nn(ordered, columns).astype(bf16).reshape(tensor, chunk, model)
-    pieces = exchange(frozen, "tensor")
-
-    grad_b_part = dot_nn(weighted.astype(bf16), late[:, :, width:].reshape(span, -1))
+    columns_early = assembled(early, after((rising[: fsdp // 2 + 1], falling[: fsdp // 2 + 1]), y))
+    product_early = dot_nn(ordered, columns_early).astype(bf16).reshape(tensor, chunk, -1)
+    pieces_early = pieces_of(product_early)
+    parts = over_groups(pieces_early)
+    arrived = after(arrived, pieces_early)
+    sums = sum(part[: tensor * (rank + 8)] for part in arrived.values()).reshape(tensor, rank + 8, chunk)
+    by_source = jnp.stack([arrived[k][tensor * (rank + 8) :] for k in range(tensor)])
+    order = [sender(mine, k, tensor) for k in range(tensor)]
+    block_index = jnp.arange(tensor)
+    rank_rows = sum(
+        jnp.where((block_index == order[k])[:, None, None], by_source[k][None], 0.0) for k in range(tensor)
+    )
+    scale = lax.rsqrt(sums[:, rank] / inner_width + epsilon)
+    adapter = sums[:, :rank].astype(bf16)
+    factor = 2.0 / math.sqrt(chunk * context * tensor * fsdp)
+    weighted = (factor * scale[:, None, :] * adapter.astype(f32)).transpose(1, 0, 2).reshape(rank, -1)
+    grad_rows = (factor * scale[:, None, :] * rank_rows).transpose(1, 0, 2).reshape(rank, -1)
+
+    grad_b_part = dot_nn(weighted.astype(bf16), turned.reshape(span, -1))
     grad_a_part = dot_nn(grad_rows.astype(bf16), flat)
-    both = spread(jnp.concatenate([grad_a_part, grad_b_part], axis=1), ("context", "fsdp"), context * fsdp)
-    both = jnp.sum(both, axis=0)
+    payload = jnp.concatenate([grad_a_part, grad_b_part], axis=1).astype(bf16)
+    both = spread(payload, ("context", "fsdp"), context * fsdp)
+    both = jnp.sum(both.astype(f32), axis=0)
     grad_a = both[:, :width].T
     grad_b = spread(both[:, width:], "tensor", tensor).transpose(1, 0, 2).reshape(rank, model)
 
+    if rest:
+        columns_rest = assembled(rest, after((rising, falling), (payload, pieces_early)))
+        product_rest = dot_nn(ordered, columns_rest).astype(bf16).reshape(tensor, chunk, -1)
+        parts = parts + over_groups(pieces_of(product_rest))
     own_scale = lax.dynamic_index_in_dim(scale, mine, 0, keepdims=False)
     own_adapter = lax.dynamic_index_in_dim(adapter, mine, 0, keepdims=False)
-    summed = jnp.sum(pieces.astype(f32), axis=0) + 2.0 * dot_tn(own_adapter, adapter_up)
-    mixed = (own_scale[:, None] * summed).astype(bf16)
+    spot = jnp.reshape(lax.axis_index("fsdp"), (1,)).astype(jnp.int32)
+    in_vmem = pl.BlockSpec(memory_space=pltpu.VMEM)
+    mixed = pl.pallas_call(
+        functools.partial(mixed_body, fsdp, tensor, (early, rest)),
+        in_specs=[pl.BlockSpec(memory_space=pltpu.SMEM)] + [in_vmem] * (3 + len(parts)),
+        out_specs=in_vmem,
+        out_shape=sds((chunk, model), bf16),
+        compiler_params=vmem,
+        name="mixed_rows",
+    )(spot, own_scale[:, None], own_adapter, adapter_up, *parts)
     return (mixed[None], grad_a, grad_b)
 
 

time: 255 us -> 196 us (0.77)
  waiting for transfers between devices: 137 us -> 69.2 us
  starting transfers between devices: 32.3 us -> 53.8 us
  local copies, waits for them, and re-layouts: 38.8 us -> 21.2 us
  Pallas kernels: 13.7 us -> 24.2 us
  blocking collectives: 8.17 us -> 0 us
    all_to_all x7 -> x5, waiting for transfers between devices: 137 us -> 22.1 us  [exchange(): return lax.all_to_all(value, axis, split_axis=0, concat_axis=0, tiled=False)]
    ppermute x1 -> x18, waiting for transfers between devices: 0.01 us -> 45.5 us  [the longest x7 32.7 us: along(): lax.ppermute(value, axis, [(i, i + step) for i in range(count) if 0 <= i...]
    ppermute x1 -> x18, starting transfers between devices: 0.07 us -> 30.1 us  [the longest x7 17.7 us: along(): lax.ppermute(value, axis, [(i, i + step) for i in range(count) if 0 <= i...]
    pallas_call x1 -> x6, Pallas kernels: 8.34 us -> 18.9 us  [the longest x3 7.19 us: packed_for(): pl.pallas_call(functools.partial(pack_body, sizes, shared_sizes), out_sha...]
    all_to_all x7 -> x5, starting transfers between devices: 30.8 us -> 21.4 us  [exchange(): return lax.all_to_all(value, axis, split_axis=0, concat_axis=0, tiled=False)]
    all_to_all x1 -> x0, blocking collectives: 8.17 us -> none  [exchange(): return lax.all_to_all(value, axis, split_axis=0, concat_axis=0, tiled=False)]
    add x0 -> x4, other arithmetic: none -> 6.32 us  [the longest x3 5.51 us: assembled(): held = [own_half if k == 0 else ends[1][k] + ends[0][fsdp - k] for k in ks]]
    another operation x5 -> x0, local copies, waits for them, and re-layouts: 6.23 us -> none  [by_group(): return values.reshape(values.shape[0], tensor, -1).transpose(1, 0, 2)]
  transfers between devices with their start and end apart: 9 -> 24, of which waited for: 5 -> 11; matrix products, arithmetic and copies ran while one was open for 18% -> 14% of each run, Pallas kernels for 5% -> 10%
where the time goes in v2:
time: 196 us; the launch traced here: 194 us
  waiting for transfers between devices  69.2 us (35%)
  starting transfers between devices  53.8 us (27%)
  Pallas kernels  24.2 us (12%)
  local copies, waits for them, and re-layouts  21.2 us (11%)
  other arithmetic  13.4 us (7%)
  matrix products  11.3 us (6%)
    ppermute x7, waiting for transfers between devices, along(): lax.ppermute(value, axis, [(i, i + step) for i in range(count) if 0 <= i...  32.7 us
    all_to_all x5, waiting for transfers between devices, exchange(): return lax.all_to_all(value, axis, split_axis=0, concat_axis=0, tiled=False)  22.1 us
    all_to_all x5, starting transfers between devices, exchange(): return lax.all_to_all(value, axis, split_axis=0, concat_axis=0, tiled=False)  21.4 us
    ppermute x7, starting transfers between devices, along(): lax.ppermute(value, axis, [(i, i + step) for i in range(count) if 0 <= i...  17.7 us
    unnamed x55, local copies, waits for them, and re-layouts  13.2 us
    ppermute x9, waiting for transfers between devices, hop(): lax.ppermute(value, axis, [(i, partner(i, step, count)) for i in range(co...  12.8 us
    ppermute x9, starting transfers between devices, hop(): lax.ppermute(value, axis, [(i, partner(i, step, count)) for i in range(co...  12 us
    dot_general x4, matrix products, dot_nn(): return jnp.dot(a, b, precision=precision, preferred_element_type=f32)  9.98 us
  transfers between devices with their start and end apart: 24, of which 11 were waited for; matrix products, arithmetic and copies ran while one was open for 14% of the time, Pallas kernels for 10%

profile of v2, /device:TPU:0, one launch (start us, length us, event | category | flops | bytes accessed | tf_op | source)
XLA Modules:
  0.0 194.3 jit_solution(17087426981977326175)
XLA Ops:
  2.2 2.7 %shard_map.157 = bf16[4,128,1664]{2,1,0:T(8,128)(2,1)} custom-call(bf16[128,5120]{1,0:T(8,128)(2,1)} %bitcast.65, bf16[128,80]{1,0:T(8,128)(2,1)} %bitcast.74, bf16[128,256]{1,0:T(8,128)(2,1)} %bitcast.75), custom_call_target="tpu_custom_call" | custom-call | tf_op jit(solution)/shard_map/pallas_call | solution.py:68
  4.9 5.2 %all-to-all-start = ((bf16[4,128,1664]{2,1,0:T(8,128)(2,1)}), bf16[4,128,1664]{2,1,0:T(8,128)(2,1)S(1)}, u32[]{:S(2)}, u32[]{:S(2)}) async-start(bf16[4,128,1664]{2,1,0:T(8,128)(2,1)} %shard_map.157), calls=%async_computation | async-start | bytes 3407872 | tf_op jit(solution)/shard_map/all_to_all | solution.py:19
  11.2 4.4 %collective-permute-start.5 = (bf16[640,640]{1,0:T(8,128)(2,1)}, bf16[640,640]{1,0:T(8,128)(2,1)}, u32[]{:S(2)}, u32[]{:S(2)}) collective-permute-start(bf16[640,640]{1,0:T(8,128)(2,1)} %constant_dynamic-slice_fusion.1), channel_id=1, source_target_pairs={{0,1},{1,2},{2,3},{4,5},{5,6},{6,7},{8,9},{9,10},{10,11},{12,13},{... | collective-permute-start | bytes 2457608 | tf_op jit(solution)/shard_map/ppermute | solution.py:44
  17.1 15.3 %collective-permute-done.5 = bf16[640,640]{1,0:T(8,128)(2,1)} collective-permute-done((bf16[640,640]{1,0:T(8,128)(2,1)}, bf16[640,640]{1,0:T(8,128)(2,1)}, u32[]{:S(2)}, u32[]{:S(2)}) %collective-permute-start.5) | collective-permute-done | bytes 819232 | tf_op jit(solution)/shard_map/ppermute | solution.py:44
  32.3 5.1 %collective-permute-done.6 = bf16[640,640]{1,0:T(8,128)(2,1)} collective-permute-done((bf16[640,640]{1,0:T(8,128)(2,1)}, bf16[640,640]{1,0:T(8,128)(2,1)}, u32[]{:S(2)}, u32[]{:S(2)}) %collective-permute-start.6) | collective-permute-done | bytes 819232 | tf_op jit(solution)/shard_map/ppermute | solution.py:44
  37.4 3.4 %collective-permute-start.7 = (bf16[640,640]{1,0:T(8,128)(2,1)}, bf16[640,640]{1,0:T(8,128)(2,1)}, u32[]{:S(2)}, u32[]{:S(2)}) collective-permute-start(bf16[640,640]{1,0:T(8,128)(2,1)} %collective-permute-done.5), channel_id=1, source_target_pairs={{0,1},{1,2},{2,3},{4,5},{5,6},{6,7},{8,9},{9,10},{10,11},{12,13},{... | collective-permute-start | bytes 2457608 | tf_op jit(solution)/shard_map/ppermute | solution.py:44
  44.2 5.4 %span_states.1 = (bf16[4,128,1280]{2,1,0:T(8,128)(2,1)S(1)}, bf16[4,128,256]{2,1,0:T(8,128)(2,1)S(1)}, f32[4,128,128]{2,1,0:T(8,128)S(1)}, f32[4,128,128]{2,1,0:...) custom-call(bf16[4,128,1664]{2,1,0:T(8,128)(2,1)S(1)} %all-to-all-done.raw, ...), custom_call_target="tpu_custom_call" | custom-call | tf_op jit(solution)/shard_map/span_states/pallas_call | solution.py:292
  52.9 2.3 %collective-permute-start.1 = (f32[128,1280]{1,0:T(8,128)}, f32[128,1280]{1,0:T(8,128)S(1)}, u32[]{:S(2)}, u32[]{:S(2)}) collective-permute-start(f32[128,1280]{1,0:T(8,128)} %get-tuple-element.31), channel_id=1, source_target_pairs={{0,16},{1,17},{2,18},{3,19},{4,20},{5,21},{6,22},{7,23},{8,24},{9,... | collective-permute-start | bytes 1966088 | tf_op jit(solution)/shard_map/ppermute | solution.py:222
  61.2 7.0 %span_recurrence.1.y_in = f32[4,128,1280]{2,1,0:T(8,128)S(1)} custom-call(bf16[4,128,1280]{2,1,0:T(8,128)(2,1)S(1)} %copy-done.6, bf16[4,128,256]{2,1,0:T(8,128)(2,1)S(1)} %copy-done.9, f32[4,128,128]{2,1,0:T(8,128)S(1)} %copy-done.11, f32[4,128,128]{2,1,0:T(8,128)S(1)} %copy-done.13, f32[4,24,128]{2,1,0:T(8,128)S(1)} %get-tuple-element.30.cumt_in, ...), custom_call_target="tpu_custom_call" | custom-call | tf_op jit(solution)/shard_map/span_recurrence/pallas_call | solution.py:308
  68.3 2.5 %add.88 = bf16[640,640]{1,0:T(8,128)(2,1)S(1)} add(bf16[640,640]{1,0:T(8,128)(2,1)} %collective-permute-done.8, bf16[640,640]{1,0:T(8,128)(2,1)} %collective-permute-done.7) | non-fusion elementwise | flops 409600 | bytes 2457600 | tf_op jit(solution)/shard_map/add | solution.py:328
  70.8 2.8 %pad_maximum_fusion = bf16[640,1280]{1,0:T(8,128)(2,1)} fusion(bf16[640,640]{1,0:T(8,128)(2,1)S(1)} %add.88, bf16[640,640]{1,0:T(8,128)(2,1)} %constant_dynamic-slice_fusion.1), kind=kLoop, calls=%fused_computation.16 | loop fusion | flops 3276800 | bytes 3276800 | tf_op jit(solution)/shard_map/concatenate | solution.py:329
  74.0 2.5 %shard_map.158 = bf16[4,128,1280]{2,1,0:T(8,128)(2,1)} custom-call(bf16[128,5120]{1,0:T(8,128)(2,1)} %bitcast.66), custom_call_target="tpu_custom_call" | custom-call | tf_op jit(solution)/shard_map/pallas_call | solution.py:68
  76.5 4.0 %all-to-all-start.1 = ((bf16[4,128,1280]{2,1,0:T(8,128)(2,1)}), bf16[4,128,1280]{2,1,0:T(8,128)(2,1)S(1)}, u32[]{:S(2)}, u32[]{:S(2)}) async-start(bf16[4,128,1280]{2,1,0:T(8,128)(2,1)} %shard_map.158), calls=%async_computation.1 | async-start | bytes 2621440 | tf_op jit(solution)/shard_map/all_to_all | solution.py:19
  80.4 2.0 %shard_map.159 = bf16[4,128,640]{2,1,0:T(8,128)(2,1)} custom-call(bf16[128,2560]{1,0:T(8,128)(2,1)} %bitcast.64), custom_call_target="tpu_custom_call" | custom-call | tf_op jit(solution)/shard_map/pallas_call | solution.py:68
  85.5 11.7 %all-to-all-done.1.gate = bf16[4,128,1280]{2,1,0:T(8,128)(2,1)S(1)} async-done(((bf16[4,128,1280]{2,1,0:T(8,128)(2,1)}), bf16[4,128,1280]{2,1,0:T(8,128)(2,1)S(1)}, u32[]{:S(2)}, u32[]{:S(2)}) %all-to-all-start.1) | async-done | bytes 1310752 | tf_op jit(solution)/shard_map/all_to_all | solution.py:19
  98.2 1.7 copy-done.2
  101.3 2.0 %span_gating.1 = (bf16[4,128,1280]{2,1,0:T(8,128)(2,1)S(1)}, f32[4,24,128]{2,1,0:T(8,128)S(1)}) custom-call(f32[4,128,1280]{2,1,0:T(8,128)S(1)} %copy-done.2, bf16[4,128,1280]{2,1,0:T(8,128)(2,1)S(1)} %copy-done.4, f32[1,1280]{1,0:T(1,128)S(1)} %broadcast_in_dim.96.gain, bf16[16,1280]{1,0:T(8,128)(2,1)S(1)} %bitcast.63), custom_call_target="tpu_custom_call" | custom-call | tf_op jit(solution)/shard_map/span_gating/pallas_call | solution.py:335
  105.4 4.2 %all-to-all-start.2 = ((bf16[4,128,640]{2,1,0:T(8,128)(2,1)}), bf16[4,128,640]{2,1,0:T(8,128)(2,1)}, u32[]{:S(2)}, u32[]{:S(2)}) async-start(bf16[4,128,640]{2,1,0:T(8,128)(2,1)} %shard_map.159), calls=%async_computation.2 | async-start | bytes 1310720 | tf_op jit(solution)/shard_map/all_to_all | solution.py:19
  109.5 4.7 %collective-permute-start.13 = (bf16[640,640]{1,0:T(8,128)(2,1)}, bf16[640,640]{1,0:T(8,128)(2,1)S(1)}, u32[]{:S(2)}, u32[]{:S(2)}) collective-permute-start(bf16[640,640]{1,0:T(8,128)(2,1)} %collective-permute-done.7), channel_id=1, source_target_pairs={{0,1},{1,2},{2,3},{4,5},{5,6},{6,7},{8,9},{9,10},{10,11},{12,13},{... | collective-permute-start | bytes 2457608 | tf_op jit(solution)/shard_map/ppermute | solution.py:44
  115.7 2.9 %collective-permute-start.4 = (f32[112,128]{1,0:T(8,128)S(1)}, f32[112,128]{1,0:T(8,128)S(1)}, u32[]{:S(2)}, u32[]{:S(2)}) collective-permute-start(f32[112,128]{1,0:T(8,128)S(1)} %pad_maximum_fusion.6), channel_id=1, source_target_pairs={{0,12},{4,8},{8,4},{12,0},{1,13},{5,9},{9,5},{13,1},{2,14},{6,10},... | collective-permute-start | bytes 172040 | tf_op jit(solution)/shard_map/ppermute | solution.py:35
  118.7 3.5 %fusion.15 = bf16[512,1280]{1,0:T(8,128)(2,1)S(1)} fusion(bf16[640,1280]{1,0:T(8,128)(2,1)} %collective-permute-done.9, bf16[640,640]{1,0:T(8,128)(2,1)S(1)} %copy-done.16, bf16[640,640]{1,0:T(8,128)(2,1)} %constant_dynamic-slice_fusion.1, bf16[512,640]{1,0:T(8,128)(2,1)S(1)} %get-tuple-element.60, bf16[512,640]{1,0:T(8,128)(2,1)S(1)} %get-tuple-element.59), kind=kOutput, calls=%fused_computation.13 | convolution fusion | flops 1690828800 | bytes 5898240 | tf_op jit(solution)/shard_map/dot_general | solution.py:87
  123.2 7.5 %collective-permute-done.13 = bf16[640,640]{1,0:T(8,128)(2,1)S(1)} collective-permute-done((bf16[640,640]{1,0:T(8,128)(2,1)}, bf16[640,640]{1,0:T(8,128)(2,1)S(1)}, u32[]{:S(2)}, u32[]{:S(2)}) %collective-permute-start.13) | collective-permute-done | bytes 819232 | tf_op jit(solution)/shard_map/ppermute | solution.py:44
  130.7 4.1 %collective-permute-done.14 = bf16[640,640]{1,0:T(8,128)(2,1)S(1)} collective-permute-done((bf16[640,640]{1,0:T(8,128)(2,1)}, bf16[640,640]{1,0:T(8,128)(2,1)S(1)}, u32[]{:S(2)}, u32[]{:S(2)}) %collective-permute-start.14) | collective-permute-done | bytes 819232 | tf_op jit(solution)/shard_map/ppermute | solution.py:44
  144.0 4.1 %all-to-all-start.3 = ((bf16[8,16,1920]{2,1,0:T(8,128)(2,1)}), bf16[8,16,1920]{2,1,0:T(8,128)(2,1)}, u32[]{:S(2)}, u32[]{:S(2)}) async-start(bf16[8,16,1920]{2,1,0:T(8,128)(2,1)} %broadcast_in_dim.108), calls=%async_computation.3 | async-start | bytes 983040 | tf_op jit(solution)/shard_map/all_to_all | solution.py:19
  148.1 2.6 %collective-permute-start.10 = (bf16[128,1280]{1,0:T(8,128)(2,1)}, bf16[128,1280]{1,0:T(8,128)(2,1)S(1)}, u32[]{:S(2)}, u32[]{:S(2)}) collective-permute-start(bf16[128,1280]{1,0:T(8,128)(2,1)} %get-tuple-element.55), channel_id=1, source_target_pairs={{0,12},{4,8},{8,4},{12,0},{1,13},{5,9},{9,5},{13,1},{2,14},{6,10},... | collective-permute-start | bytes 983048 | tf_op jit(solution)/shard_map/ppermute | solution.py:35
  151.8 10.4 %all-to-all-done.3 = bf16[8,16,1920]{2,1,0:T(8,128)(2,1)} async-done(((bf16[8,16,1920]{2,1,0:T(8,128)(2,1)}), bf16[8,16,1920]{2,1,0:T(8,128)(2,1)}, u32[]{:S(2)}, u32[]{:S(2)}) %all-to-all-start.3) | async-done | bytes 491552 | tf_op jit(solution)/shard_map/all_to_all | solution.py:19
  164.0 4.0 %all-to-all-start.4 = ((f32[4,16,640]{2,1,0:T(8,128)}), f32[4,16,640]{2,1,0:T(8,128)}, u32[]{:S(2)}, u32[]{:S(2)}) async-start(f32[4,16,640]{2,1,0:T(8,128)} %broadcast_in_dim.109), calls=%async_computation.4 | async-start | bytes 327680 | tf_op jit(solution)/shard_map/all_to_all | solution.py:19
  168.0 4.1 %fusion.12 = bf16[512,1280]{1,0:T(8,128)(2,1)S(1)} fusion(bf16[640,1280]{1,0:T(8,128)(2,1)} %collective-permute-done.15, bf16[640,640]{1,0:T(8,128)(2,1)} %copy-done.18, bf16[640,640]{1,0:T(8,128)(2,1)} %copy-done.17, bf16[512,640]{1,0:T(8,128)(2,1)} %copy-done.20, bf16[512,640]{1,0:T(8,128)(2,1)} %copy-done.19), kind=kOutput, calls=%fused_computation.12 | convolution fusion | flops 1690828800 | bytes 5898240 | tf_op jit(solution)/shard_map/dot_general | solution.py:87
  173.2 2.9 %collective-permute-start.16 = (bf16[128,1280]{1,0:T(8,128)(2,1)}, bf16[128,1280]{1,0:T(8,128)(2,1)}, u32[]{:S(2)}, u32[]{:S(2)}) collective-permute-start(bf16[128,1280]{1,0:T(8,128)(2,1)} %get-tuple-element.53), channel_id=1, source_target_pairs={{0,12},{4,8},{8,4},{12,0},{1,13},{5,9},{9,5},{13,1},{2,14},{6,10},... | collective-permute-start | bytes 983048 | tf_op jit(solution)/shard_map/ppermute | solution.py:35
  178.9 6.1 %collective-permute-done.16.refs_5_ = bf16[128,1280]{1,0:T(8,128)(2,1)} collective-permute-done((bf16[128,1280]{1,0:T(8,128)(2,1)}, bf16[128,1280]{1,0:T(8,128)(2,1)}, u32[]{:S(2)}, u32[]{:S(2)}) %collective-permute-start.16) | collective-permute-done | bytes 327712 | tf_op jit(solution)/shard_map/ppermute | solution.py:35
  185.0 6.4 %collective-permute-done.17.refs_6_ = bf16[128,1280]{1,0:T(8,128)(2,1)} collective-permute-done((bf16[128,1280]{1,0:T(8,128)(2,1)}, bf16[128,1280]{1,0:T(8,128)(2,1)}, u32[]{:S(2)}, u32[]{:S(2)}) %collective-permute-start.17) | collective-permute-done | bytes 327712 | tf_op jit(solution)/shard_map/ppermute | solution.py:35
  191.7 2.6 %mixed_rows.1 = bf16[128,2560]{1,0:T(8,128)(2,1)} custom-call(s32[1]{0:T(128)} %bitcast.spot, f32[128,1]{1,0:T(8,128)S(1)} %copy.25.scale, bf16[16,128]{1,0:T(8,128)(2,1)S(1)} %dynamic-slice_bitcast_fusion.8.adapter, bf16[16,2560]{1,0:T(8,128)(2,1)S(1)} %copy-done.7, bf16[128,1280]{1,0:T(8,128)(2,1)S(1)} %get-tuple-element.58.refs_0_, ...), custom_call_target="tpu_custom_call" | custom-call | tf_op jit(solution)/shard_map/mixed_rows/pallas_call | solution.py:389
  (128 shorter events, 43.0 us)
Async XLA Ops:
  0.6 9.5 %copy-start = (bf16[1280,640]{1,0:T(8,128)(2,1)S(1)}, bf16[1280,640]{1,0:T(8,128)(2,1)}, u32[]{:S(2)}) copy-start(bf16[1280,640]{1,0:T(8,128)(2,1)} %param.24) | copy-start | bytes 4915204
  4.9 32.5 %all-to-all-start = ((bf16[4,128,1664]{2,1,0:T(8,128)(2,1)}), bf16[4,128,1664]{2,1,0:T(8,128)(2,1)S(1)}, u32[]{:S(2)}, u32[]{:S(2)}) async-start(bf16[4,128,1664]{2,1,0:T(8,128)(2,1)} %shard_map.157), calls=%async_computation | async-start | bytes 3407872 | tf_op jit(solution)/shard_map/all_to_all | solution.py:19
  10.1 6.9 %copy-start.21 = (f32[4,5376]{1,0:T(4,128)S(1)}, f32[4,5376]{1,0:T(4,128)}, u32[]{:S(2)}) copy-start(f32[4,5376]{1,0:T(4,128)} %param.18) | copy-start | bytes 258052
  10.1 6.9 %slice-start = ((f32[4,5376]{1,0:T(4,128)}), f32[4,256]{1,0:T(4,128)S(1)}, s32[]{:S(2)}) async-start(f32[4,5376]{1,0:T(4,128)} %param.18), calls=%async_computation.5 | async-start | bytes 8192 | tf_op jit(solution)/shard_map/slice | solution.py:286
  10.1 33.3 %copy-start.25 = (f32[20]{0:T(128)S(1)}, f32[20]{0:T(128)}, u32[]{:S(2)}) copy-start(f32[20]{0:T(128)} %param.20) | copy-start | bytes 244
  10.2 45.0 %copy-start.24 = (f32[20]{0:T(128)S(1)}, f32[20]{0:T(128)}, u32[]{:S(2)}) copy-start(f32[20]{0:T(128)} %param.22) | copy-start | bytes 244
  11.2 21.2 %collective-permute-start.5 = (bf16[640,640]{1,0:T(8,128)(2,1)}, bf16[640,640]{1,0:T(8,128)(2,1)}, u32[]{:S(2)}, u32[]{:S(2)}) collective-permute-start(bf16[640,640]{1,0:T(8,128)(2,1)} %constant_dynamic-slice_fusion.1), channel_id=1, source_target_pairs={{0,1},{1,2},{2,3},{4,5},{5,6},{6,7},{8,9},{9,10},{10,11},{12,13},{... | collective-permute-start | bytes 2457608 | tf_op jit(solution)/shard_map/ppermute | solution.py:44
  15.6 21.8 %collective-permute-start.6 = (bf16[640,640]{1,0:T(8,128)(2,1)}, bf16[640,640]{1,0:T(8,128)(2,1)}, u32[]{:S(2)}, u32[]{:S(2)}) collective-permute-start(bf16[640,640]{1,0:T(8,128)(2,1)} %constant_dynamic-slice_fusion.1), channel_id=1, source_target_pairs={{1,0},{2,1},{3,2},{5,4},{6,5},{7,6},{9,8},{10,9},{11,10},{13,12},{... | collective-permute-start | bytes 2457608 | tf_op jit(solution)/shard_map/ppermute | solution.py:44
  37.4 30.9 %collective-permute-start.7 = (bf16[640,640]{1,0:T(8,128)(2,1)}, bf16[640,640]{1,0:T(8,128)(2,1)}, u32[]{:S(2)}, u32[]{:S(2)}) collective-permute-start(bf16[640,640]{1,0:T(8,128)(2,1)} %collective-permute-done.5), channel_id=1, source_target_pairs={{0,1},{1,2},{2,3},{4,5},{5,6},{6,7},{8,9},{9,10},{10,11},{12,13},{... | collective-permute-start | bytes 2457608 | tf_op jit(solution)/shard_map/ppermute | solution.py:44
  40.8 27.5 %collective-permute-start.8 = (bf16[640,640]{1,0:T(8,128)(2,1)}, bf16[640,640]{1,0:T(8,128)(2,1)}, u32[]{:S(2)}, u32[]{:S(2)}) collective-permute-start(bf16[640,640]{1,0:T(8,128)(2,1)} %collective-permute-done.6), channel_id=1, source_target_pairs={{1,0},{2,1},{3,2},{5,4},{6,5},{7,6},{9,8},{10,9},{11,10},{13,12},{... | collective-permute-start | bytes 2457608 | tf_op jit(solution)/shard_map/ppermute | solution.py:44
  42.1 2.1 %collective-permute-start = (bf16[8,1536]{1,0:T(8,128)(2,1)S(1)}, bf16[8,1536]{1,0:T(8,128)(2,1)S(1)}, u32[]{:S(2)}, u32[]{:S(2)}) collective-permute-start(bf16[8,1536]{1,0:T(8,128)(2,1)S(1)} %slice_bitcast_fusion.1), channel_id=1, source_target_pairs={{0,16},{1,17},{2,18},{3,19},{4,20},{5,21},{6,22},{7,23},{8,24},{9,... | collective-permute-start | bytes 73736 | tf_op jit(solution)/shard_map/ppermute | solution.py:44
  52.9 4.2 %collective-permute-start.1 = (f32[128,1280]{1,0:T(8,128)}, f32[128,1280]{1,0:T(8,128)S(1)}, u32[]{:S(2)}, u32[]{:S(2)}) collective-permute-start(f32[128,1280]{1,0:T(8,128)} %get-tuple-element.31), channel_id=1, source_target_pairs={{0,16},{1,17},{2,18},{3,19},{4,20},{5,21},{6,22},{7,23},{8,24},{9,... | collective-permute-start | bytes 1966088 | tf_op jit(solution)/shard_map/ppermute | solution.py:222
  73.6 42.1 %collective-permute-start.9 = (bf16[640,1280]{1,0:T(8,128)(2,1)}, bf16[640,1280]{1,0:T(8,128)(2,1)}, u32[]{:S(2)}, u32[]{:S(2)}) collective-permute-start(bf16[640,1280]{1,0:T(8,128)(2,1)} %pad_maximum_fusion), channel_id=1, source_target_pairs={{0,16},{16,0},{1,17},{17,1},{2,18},{18,2},{3,19},{19,3},{4,20},{20... | collective-permute-start | bytes 4915208 | tf_op jit(solution)/shard_map/ppermute | solution.py:332
  76.4 7.7 %copy-start.7 = (bf16[16,2560]{1,0:T(8,128)(2,1)S(1)}, bf16[16,2560]{1,0:T(8,128)(2,1)}, u32[]{:S(2)}) copy-start(bf16[16,2560]{1,0:T(8,128)(2,1)} %up.1) | copy-start | bytes 245764
  76.5 20.7 %all-to-all-start.1 = ((bf16[4,128,1280]{2,1,0:T(8,128)(2,1)}), bf16[4,128,1280]{2,1,0:T(8,128)(2,1)S(1)}, u32[]{:S(2)}, u32[]{:S(2)}) async-start(bf16[4,128,1280]{2,1,0:T(8,128)(2,1)} %shard_map.158), calls=%async_computation.1 | async-start | bytes 2621440 | tf_op jit(solution)/shard_map/all_to_all | solution.py:19
  80.4 17.8 %copy-start.14 = (bf16[1280,16]{0,1:T(8,128)(2,1)S(1)}, bf16[1280,16]{0,1:T(8,128)(2,1)}, u32[]{:S(2)}) copy-start(bf16[1280,16]{0,1:T(8,128)(2,1)} %param.25) | copy-start | bytes 122884
  103.3 35.9 %collective-permute-start.2 = (f32[112,128]{1,0:T(8,128)S(1)}, f32[112,128]{1,0:T(8,128)S(1)}, u32[]{:S(2)}, u32[]{:S(2)}) collective-permute-start(f32[112,128]{1,0:T(8,128)S(1)} %pad_maximum_fusion.6), channel_id=1, source_target_pairs={{0,4},{4,0},{8,12},{12,8},{1,5},{5,1},{9,13},{13,9},{2,6},{6,2},{1... | collective-permute-start | bytes 172040 | tf_op jit(solution)/shard_map/ppermute | solution.py:35
  104.8 34.4 %collective-permute-start.3 = (f32[112,128]{1,0:T(8,128)S(1)}, f32[112,128]{1,0:T(8,128)}, u32[]{:S(2)}, u32[]{:S(2)}) collective-permute-start(f32[112,128]{1,0:T(8,128)S(1)} %pad_maximum_fusion.6), channel_id=1, source_target_pairs={{0,8},{4,12},{8,0},{12,4},{1,9},{5,13},{9,1},{13,5},{2,10},{6,14},... | collective-permute-start | bytes 172040 | tf_op jit(solution)/shard_map/ppermute | solution.py:35
  105.4 35.4 %all-to-all-start.2 = ((bf16[4,128,640]{2,1,0:T(8,128)(2,1)}), bf16[4,128,640]{2,1,0:T(8,128)(2,1)}, u32[]{:S(2)}, u32[]{:S(2)}) async-start(bf16[4,128,640]{2,1,0:T(8,128)(2,1)} %shard_map.159), calls=%async_computation.2 | async-start | bytes 1310720 | tf_op jit(solution)/shard_map/all_to_all | solution.py:19
  109.5 9.1 %copy-start.16 = (bf16[640,640]{1,0:T(8,128)(2,1)S(1)}, bf16[640,640]{1,0:T(8,128)(2,1)}, u32[]{:S(2)}) copy-start(bf16[640,640]{1,0:T(8,128)(2,1)} %copy-done.15) | copy-start | bytes 2457604
  109.5 21.1 %collective-permute-start.13 = (bf16[640,640]{1,0:T(8,128)(2,1)}, bf16[640,640]{1,0:T(8,128)(2,1)S(1)}, u32[]{:S(2)}, u32[]{:S(2)}) collective-permute-start(bf16[640,640]{1,0:T(8,128)(2,1)} %collective-permute-done.7), channel_id=1, source_target_pairs={{0,1},{1,2},{2,3},{4,5},{5,6},{6,7},{8,9},{9,10},{10,11},{12,13},{... | collective-permute-start | bytes 2457608 | tf_op jit(solution)/shard_map/ppermute | solution.py:44
  114.3 20.5 %collective-permute-start.14 = (bf16[640,640]{1,0:T(8,128)(2,1)}, bf16[640,640]{1,0:T(8,128)(2,1)S(1)}, u32[]{:S(2)}, u32[]{:S(2)}) collective-permute-start(bf16[640,640]{1,0:T(8,128)(2,1)} %collective-permute-done.8), channel_id=1, source_target_pairs={{1,0},{2,1},{3,2},{5,4},{6,5},{7,6},{9,8},{10,9},{11,10},{13,12},{... | collective-permute-start | bytes 2457608 | tf_op jit(solution)/shard_map/ppermute | solution.py:44
  115.7 23.5 %collective-permute-start.4 = (f32[112,128]{1,0:T(8,128)S(1)}, f32[112,128]{1,0:T(8,128)S(1)}, u32[]{:S(2)}, u32[]{:S(2)}) collective-permute-start(f32[112,128]{1,0:T(8,128)S(1)} %pad_maximum_fusion.6), channel_id=1, source_target_pairs={{0,12},{4,8},{8,4},{12,0},{1,13},{5,9},{9,5},{13,1},{2,14},{6,10},... | collective-permute-start | bytes 172040 | tf_op jit(solution)/shard_map/ppermute | solution.py:35
  139.9 28.1 %collective-permute-start.15 = (bf16[640,1280]{1,0:T(8,128)(2,1)}, bf16[640,1280]{1,0:T(8,128)(2,1)}, u32[]{:S(2)}, u32[]{:S(2)}) collective-permute-start(bf16[640,1280]{1,0:T(8,128)(2,1)} %pad_maximum_fusion.1), channel_id=1, source_target_pairs={{0,16},{16,0},{1,17},{17,1},{2,18},{18,2},{3,19},{19,3},{4,20},{20... | collective-permute-start | bytes 4915208 | tf_op jit(solution)/shard_map/ppermute | solution.py:332
  144.0 18.2 %all-to-all-start.3 = ((bf16[8,16,1920]{2,1,0:T(8,128)(2,1)}), bf16[8,16,1920]{2,1,0:T(8,128)(2,1)}, u32[]{:S(2)}, u32[]{:S(2)}) async-start(bf16[8,16,1920]{2,1,0:T(8,128)(2,1)} %broadcast_in_dim.108), calls=%async_computation.3 | async-start | bytes 983040 | tf_op jit(solution)/shard_map/all_to_all | solution.py:19
  148.1 28.5 %collective-permute-start.10 = (bf16[128,1280]{1,0:T(8,128)(2,1)}, bf16[128,1280]{1,0:T(8,128)(2,1)S(1)}, u32[]{:S(2)}, u32[]{:S(2)}) collective-permute-start(bf16[128,1280]{1,0:T(8,128)(2,1)} %get-tuple-element.55), channel_id=1, source_target_pairs={{0,12},{4,8},{8,4},{12,0},{1,13},{5,9},{9,5},{13,1},{2,14},{6,10},... | collective-permute-start | bytes 983048 | tf_op jit(solution)/shard_map/ppermute | solution.py:35
  150.8 28.1 %collective-permute-start.11 = (bf16[128,1280]{1,0:T(8,128)(2,1)}, bf16[128,1280]{1,0:T(8,128)(2,1)S(1)}, u32[]{:S(2)}, u32[]{:S(2)}) collective-permute-start(bf16[128,1280]{1,0:T(8,128)(2,1)} %get-tuple-element.56), channel_id=1, source_target_pairs={{0,8},{4,12},{8,0},{12,4},{1,9},{5,13},{9,1},{13,5},{2,10},{6,14},... | collective-permute-start | bytes 983048 | tf_op jit(solution)/shard_map/ppermute | solution.py:35
  151.3 27.6 %collective-permute-start.12 = (bf16[128,1280]{1,0:T(8,128)(2,1)}, bf16[128,1280]{1,0:T(8,128)(2,1)S(1)}, u32[]{:S(2)}, u32[]{:S(2)}) collective-permute-start(bf16[128,1280]{1,0:T(8,128)(2,1)} %get-tuple-element.57), channel_id=1, source_target_pairs={{0,4},{4,0},{8,12},{12,8},{1,5},{5,1},{9,13},{13,9},{2,6},{6,2},{1... | collective-permute-start | bytes 983048 | tf_op jit(solution)/shard_map/ppermute | solution.py:35
  164.0 13.3 %all-to-all-start.4 = ((f32[4,16,640]{2,1,0:T(8,128)}), f32[4,16,640]{2,1,0:T(8,128)}, u32[]{:S(2)}, u32[]{:S(2)}) async-start(f32[4,16,640]{2,1,0:T(8,128)} %broadcast_in_dim.109), calls=%async_computation.4 | async-start | bytes 327680 | tf_op jit(solution)/shard_map/all_to_all | solution.py:19
  173.2 11.8 %collective-permute-start.16 = (bf16[128,1280]{1,0:T(8,128)(2,1)}, bf16[128,1280]{1,0:T(8,128)(2,1)}, u32[]{:S(2)}, u32[]{:S(2)}) collective-permute-start(bf16[128,1280]{1,0:T(8,128)(2,1)} %get-tuple-element.53), channel_id=1, source_target_pairs={{0,12},{4,8},{8,4},{12,0},{1,13},{5,9},{9,5},{13,1},{2,14},{6,10},... | collective-permute-start | bytes 983048 | tf_op jit(solution)/shard_map/ppermute | solution.py:35
  176.0 15.4 %collective-permute-start.17 = (bf16[128,1280]{1,0:T(8,128)(2,1)}, bf16[128,1280]{1,0:T(8,128)(2,1)}, u32[]{:S(2)}, u32[]{:S(2)}) collective-permute-start(bf16[128,1280]{1,0:T(8,128)(2,1)} %get-tuple-element.52), channel_id=1, source_target_pairs={{0,8},{4,12},{8,0},{12,4},{1,9},{5,13},{9,1},{13,5},{2,10},{6,14},... | collective-permute-start | bytes 983048 | tf_op jit(solution)/shard_map/ppermute | solution.py:35
  176.6 15.1 %collective-permute-start.18 = (bf16[128,1280]{1,0:T(8,128)(2,1)}, bf16[128,1280]{1,0:T(8,128)(2,1)}, u32[]{:S(2)}, u32[]{:S(2)}) collective-permute-start(bf16[128,1280]{1,0:T(8,128)(2,1)} %get-tuple-element.51), channel_id=1, source_target_pairs={{0,4},{4,0},{8,12},{12,8},{1,5},{5,1},{9,13},{13,9},{2,6},{6,2},{1... | collective-permute-start | bytes 983048 | tf_op jit(solution)/shard_map/ppermute | solution.py:35
  (21 other events, 61.7 us)

commit v3 on v2

--- a/solution.py
+++ b/solution.py
@@ -269,7 +269,8 @@
     def over_groups(pieces):
         return [pieces[0]] + [hop(pieces[k], "tensor", k, tensor) for k in reversed(range(1, tensor))]
 
-    raw = exchange(packed_for(tensor, [input_raw[0], step_raw[0]], [state_proj_raw[0]]), "tensor")
+    packed_raw = packed_for(tensor, [input_raw[0], step_raw[0]], [state_proj_raw[0]])
+    raw = exchange(packed_raw, "tensor")
     rim = along(raw[tensor - 1, chunk - 8 :, :joint], "context", 1)
     place = lax.axis_index("context")
     packed_gate = packed_for(tensor, [gate_branch[0]], [])
@@ -312,7 +313,8 @@
         compiler_params=vmem,
         name="span_recurrence",
     )(xconv, bc, step, cum, cumt, start_state, jnp.repeat(skip_weight, head_size)[None])
-    packed_turn = after(packed_for(tensor, [cotangent[0]], []), y)
+    packed_turn = packed_for(tensor, [cotangent[0]], [])
+    packed_turn = after(packed_turn, y)
     turned = exchange(packed_turn, "tensor")
     waits = {1: raw, 2: y}
     for step_index in range(1, fsdp - 1):
@@ -381,7 +383,8 @@
     if rest:
         columns_rest = assembled(rest, after((rising, falling), (payload, pieces_early)))
         product_rest = dot_nn(ordered, columns_rest).astype(bf16).reshape(tensor, chunk, -1)
-        parts = parts + over_groups(pieces_of(product_rest))
+        pieces_rest = pieces_of(product_rest)
+        parts = parts + over_groups(pieces_rest)
     own_scale = lax.dynamic_index_in_dim(scale, mine, 0, keepdims=False)
     own_adapter = lax.dynamic_index_in_dim(adapter, mine, 0, keepdims=False)
     spot = jnp.reshape(lax.axis_index("fsdp"), (1,)).astype(jnp.int32)

time: 196 us -> 196 us (level)
  no operation moved by 1% of the time
where the time goes in v3:
time: 196 us; the launch traced here: 194 us
  waiting for transfers between devices  69.2 us (35%)
  starting transfers between devices  53.8 us (27%)
  Pallas kernels  24.2 us (12%)
  local copies, waits for them, and re-layouts  21.2 us (11%)
  other arithmetic  13.4 us (7%)
  matrix products  11.3 us (6%)
    ppermute x7, waiting for transfers between devices, along(): lax.ppermute(value, axis, [(i, i + step) for i in range(count) if 0 <= i...  32.7 us
    all_to_all x5, waiting for transfers between devices, exchange(): return lax.all_to_all(value, axis, split_axis=0, concat_axis=0, tiled=False)  22.1 us
    all_to_all x5, starting transfers between devices, exchange(): return lax.all_to_all(value, axis, split_axis=0, concat_axis=0, tiled=False)  21.4 us
    ppermute x7, starting transfers between devices, along(): lax.ppermute(value, axis, [(i, i + step) for i in range(count) if 0 <= i...  17.7 us
    unnamed x55, local copies, waits for them, and re-layouts  13.2 us
    ppermute x9, waiting for transfers between devices, hop(): lax.ppermute(value, axis, [(i, partner(i, step, count)) for i in range(co...  12.8 us
    ppermute x9, starting transfers between devices, hop(): lax.ppermute(value, axis, [(i, partner(i, step, count)) for i in range(co...  12 us
    dot_general x4, matrix products, dot_nn(): return jnp.dot(a, b, precision=precision, preferred_element_type=f32)  9.98 us
  transfers between devices with their start and end apart: 24, of which 11 were waited for; matrix products, arithmetic and copies ran while one was open for 14% of the time, Pallas kernels for 10%

profile of v3, /device:TPU:0, one launch (start us, length us, event | category | flops | bytes accessed | tf_op | source)
XLA Modules:
  0.0 194.3 jit_solution(17087426981977326175)
XLA Ops:
  2.2 2.7 %shard_map.157 = bf16[4,128,1664]{2,1,0:T(8,128)(2,1)} custom-call(bf16[128,5120]{1,0:T(8,128)(2,1)} %bitcast.65, bf16[128,80]{1,0:T(8,128)(2,1)} %bitcast.74, bf16[128,256]{1,0:T(8,128)(2,1)} %bitcast.75), custom_call_target="tpu_custom_call" | custom-call | tf_op jit(solution)/shard_map/pallas_call | solution.py:68
  4.9 5.2 %all-to-all-start = ((bf16[4,128,1664]{2,1,0:T(8,128)(2,1)}), bf16[4,128,1664]{2,1,0:T(8,128)(2,1)S(1)}, u32[]{:S(2)}, u32[]{:S(2)}) async-start(bf16[4,128,1664]{2,1,0:T(8,128)(2,1)} %shard_map.157), calls=%async_computation | async-start | bytes 3407872 | tf_op jit(solution)/shard_map/all_to_all | solution.py:19
  11.2 4.4 %collective-permute-start.5 = (bf16[640,640]{1,0:T(8,128)(2,1)}, bf16[640,640]{1,0:T(8,128)(2,1)}, u32[]{:S(2)}, u32[]{:S(2)}) collective-permute-start(bf16[640,640]{1,0:T(8,128)(2,1)} %constant_dynamic-slice_fusion.1), channel_id=1, source_target_pairs={{0,1},{1,2},{2,3},{4,5},{5,6},{6,7},{8,9},{9,10},{10,11},{12,13},{... | collective-permute-start | bytes 2457608 | tf_op jit(solution)/shard_map/ppermute | solution.py:44
  17.1 15.3 %collective-permute-done.5 = bf16[640,640]{1,0:T(8,128)(2,1)} collective-permute-done((bf16[640,640]{1,0:T(8,128)(2,1)}, bf16[640,640]{1,0:T(8,128)(2,1)}, u32[]{:S(2)}, u32[]{:S(2)}) %collective-permute-start.5) | collective-permute-done | bytes 819232 | tf_op jit(solution)/shard_map/ppermute | solution.py:44
  32.3 5.1 %collective-permute-done.6 = bf16[640,640]{1,0:T(8,128)(2,1)} collective-permute-done((bf16[640,640]{1,0:T(8,128)(2,1)}, bf16[640,640]{1,0:T(8,128)(2,1)}, u32[]{:S(2)}, u32[]{:S(2)}) %collective-permute-start.6) | collective-permute-done | bytes 819232 | tf_op jit(solution)/shard_map/ppermute | solution.py:44
  37.4 3.4 %collective-permute-start.7 = (bf16[640,640]{1,0:T(8,128)(2,1)}, bf16[640,640]{1,0:T(8,128)(2,1)}, u32[]{:S(2)}, u32[]{:S(2)}) collective-permute-start(bf16[640,640]{1,0:T(8,128)(2,1)} %collective-permute-done.5), channel_id=1, source_target_pairs={{0,1},{1,2},{2,3},{4,5},{5,6},{6,7},{8,9},{9,10},{10,11},{12,13},{... | collective-permute-start | bytes 2457608 | tf_op jit(solution)/shard_map/ppermute | solution.py:44
  44.2 5.4 %span_states.1 = (bf16[4,128,1280]{2,1,0:T(8,128)(2,1)S(1)}, bf16[4,128,256]{2,1,0:T(8,128)(2,1)S(1)}, f32[4,128,128]{2,1,0:T(8,128)S(1)}, f32[4,128,128]{2,1,0:...) custom-call(bf16[4,128,1664]{2,1,0:T(8,128)(2,1)S(1)} %all-to-all-done.raw, ...), custom_call_target="tpu_custom_call" | custom-call | tf_op jit(solution)/shard_map/span_states/pallas_call | solution.py:293
  52.9 2.3 %collective-permute-start.1 = (f32[128,1280]{1,0:T(8,128)}, f32[128,1280]{1,0:T(8,128)S(1)}, u32[]{:S(2)}, u32[]{:S(2)}) collective-permute-start(f32[128,1280]{1,0:T(8,128)} %get-tuple-element.31), channel_id=1, source_target_pairs={{0,16},{1,17},{2,18},{3,19},{4,20},{5,21},{6,22},{7,23},{8,24},{9,... | collective-permute-start | bytes 1966088 | tf_op jit(solution)/shard_map/ppermute | solution.py:222
  61.2 7.0 %span_recurrence.1.y_in = f32[4,128,1280]{2,1,0:T(8,128)S(1)} custom-call(bf16[4,128,1280]{2,1,0:T(8,128)(2,1)S(1)} %copy-done.6, bf16[4,128,256]{2,1,0:T(8,128)(2,1)S(1)} %copy-done.9, f32[4,128,128]{2,1,0:T(8,128)S(1)} %copy-done.11, f32[4,128,128]{2,1,0:T(8,128)S(1)} %copy-done.13, f32[4,24,128]{2,1,0:T(8,128)S(1)} %get-tuple-element.30.cumt_in, ...), custom_call_target="tpu_custom_call" | custom-call | tf_op jit(solution)/shard_map/span_recurrence/pallas_call | solution.py:309
  68.3 2.5 %add.88 = bf16[640,640]{1,0:T(8,128)(2,1)S(1)} add(bf16[640,640]{1,0:T(8,128)(2,1)} %collective-permute-done.8, bf16[640,640]{1,0:T(8,128)(2,1)} %collective-permute-done.7) | non-fusion elementwise | flops 409600 | bytes 2457600 | tf_op jit(solution)/shard_map/add | solution.py:330
  70.8 2.8 %pad_maximum_fusion = bf16[640,1280]{1,0:T(8,128)(2,1)} fusion(bf16[640,640]{1,0:T(8,128)(2,1)S(1)} %add.88, bf16[640,640]{1,0:T(8,128)(2,1)} %constant_dynamic-slice_fusion.1), kind=kLoop, calls=%fused_computation.16 | loop fusion | flops 3276800 | bytes 3276800 | tf_op jit(solution)/shard_map/concatenate | solution.py:331
  74.0 2.5 %shard_map.158 = bf16[4,128,1280]{2,1,0:T(8,128)(2,1)} custom-call(bf16[128,5120]{1,0:T(8,128)(2,1)} %bitcast.66), custom_call_target="tpu_custom_call" | custom-call | tf_op jit(solution)/shard_map/pallas_call | solution.py:68
  76.5 4.0 %all-to-all-start.1 = ((bf16[4,128,1280]{2,1,0:T(8,128)(2,1)}), bf16[4,128,1280]{2,1,0:T(8,128)(2,1)S(1)}, u32[]{:S(2)}, u32[]{:S(2)}) async-start(bf16[4,128,1280]{2,1,0:T(8,128)(2,1)} %shard_map.158), calls=%async_computation.1 | async-start | bytes 2621440 | tf_op jit(solution)/shard_map/all_to_all | solution.py:19
  80.4 2.0 %shard_map.159 = bf16[4,128,640]{2,1,0:T(8,128)(2,1)} custom-call(bf16[128,2560]{1,0:T(8,128)(2,1)} %bitcast.64), custom_call_target="tpu_custom_call" | custom-call | tf_op jit(solution)/shard_map/pallas_call | solution.py:68
  85.5 11.7 %all-to-all-done.1.gate = bf16[4,128,1280]{2,1,0:T(8,128)(2,1)S(1)} async-done(((bf16[4,128,1280]{2,1,0:T(8,128)(2,1)}), bf16[4,128,1280]{2,1,0:T(8,128)(2,1)S(1)}, u32[]{:S(2)}, u32[]{:S(2)}) %all-to-all-start.1) | async-done | bytes 1310752 | tf_op jit(solution)/shard_map/all_to_all | solution.py:19
  98.2 1.7 copy-done.2
  101.3 2.0 %span_gating.1 = (bf16[4,128,1280]{2,1,0:T(8,128)(2,1)S(1)}, f32[4,24,128]{2,1,0:T(8,128)S(1)}) custom-call(f32[4,128,1280]{2,1,0:T(8,128)S(1)} %copy-done.2, bf16[4,128,1280]{2,1,0:T(8,128)(2,1)S(1)} %copy-done.4, f32[1,1280]{1,0:T(1,128)S(1)} %broadcast_in_dim.96.gain, bf16[16,1280]{1,0:T(8,128)(2,1)S(1)} %bitcast.63), custom_call_target="tpu_custom_call" | custom-call | tf_op jit(solution)/shard_map/span_gating/pallas_call | solution.py:337
  105.4 4.2 %all-to-all-start.2 = ((bf16[4,128,640]{2,1,0:T(8,128)(2,1)}), bf16[4,128,640]{2,1,0:T(8,128)(2,1)}, u32[]{:S(2)}, u32[]{:S(2)}) async-start(bf16[4,128,640]{2,1,0:T(8,128)(2,1)} %shard_map.159), calls=%async_computation.2 | async-start | bytes 1310720 | tf_op jit(solution)/shard_map/all_to_all | solution.py:19
  109.5 4.7 %collective-permute-start.13 = (bf16[640,640]{1,0:T(8,128)(2,1)}, bf16[640,640]{1,0:T(8,128)(2,1)S(1)}, u32[]{:S(2)}, u32[]{:S(2)}) collective-permute-start(bf16[640,640]{1,0:T(8,128)(2,1)} %collective-permute-done.7), channel_id=1, source_target_pairs={{0,1},{1,2},{2,3},{4,5},{5,6},{6,7},{8,9},{9,10},{10,11},{12,13},{... | collective-permute-start | bytes 2457608 | tf_op jit(solution)/shard_map/ppermute | solution.py:44
  115.7 2.9 %collective-permute-start.4 = (f32[112,128]{1,0:T(8,128)S(1)}, f32[112,128]{1,0:T(8,128)S(1)}, u32[]{:S(2)}, u32[]{:S(2)}) collective-permute-start(f32[112,128]{1,0:T(8,128)S(1)} %pad_maximum_fusion.6), channel_id=1, source_target_pairs={{0,12},{4,8},{8,4},{12,0},{1,13},{5,9},{9,5},{13,1},{2,14},{6,10},... | collective-permute-start | bytes 172040 | tf_op jit(solution)/shard_map/ppermute | solution.py:35
  118.7 3.5 %fusion.15 = bf16[512,1280]{1,0:T(8,128)(2,1)S(1)} fusion(bf16[640,1280]{1,0:T(8,128)(2,1)} %collective-permute-done.9, bf16[640,640]{1,0:T(8,128)(2,1)S(1)} %copy-done.16, bf16[640,640]{1,0:T(8,128)(2,1)} %constant_dynamic-slice_fusion.1, bf16[512,640]{1,0:T(8,128)(2,1)S(1)} %get-tuple-element.60, bf16[512,640]{1,0:T(8,128)(2,1)S(1)} %get-tuple-element.59), kind=kOutput, calls=%fused_computation.13 | convolution fusion | flops 1690828800 | bytes 5898240 | tf_op jit(solution)/shard_map/dot_general | solution.py:87
  123.2 7.5 %collective-permute-done.13 = bf16[640,640]{1,0:T(8,128)(2,1)S(1)} collective-permute-done((bf16[640,640]{1,0:T(8,128)(2,1)}, bf16[640,640]{1,0:T(8,128)(2,1)S(1)}, u32[]{:S(2)}, u32[]{:S(2)}) %collective-permute-start.13) | collective-permute-done | bytes 819232 | tf_op jit(solution)/shard_map/ppermute | solution.py:44
  130.7 4.1 %collective-permute-done.14 = bf16[640,640]{1,0:T(8,128)(2,1)S(1)} collective-permute-done((bf16[640,640]{1,0:T(8,128)(2,1)}, bf16[640,640]{1,0:T(8,128)(2,1)S(1)}, u32[]{:S(2)}, u32[]{:S(2)}) %collective-permute-start.14) | collective-permute-done | bytes 819232 | tf_op jit(solution)/shard_map/ppermute | solution.py:44
  144.0 4.1 %all-to-all-start.3 = ((bf16[8,16,1920]{2,1,0:T(8,128)(2,1)}), bf16[8,16,1920]{2,1,0:T(8,128)(2,1)}, u32[]{:S(2)}, u32[]{:S(2)}) async-start(bf16[8,16,1920]{2,1,0:T(8,128)(2,1)} %broadcast_in_dim.108), calls=%async_computation.3 | async-start | bytes 983040 | tf_op jit(solution)/shard_map/all_to_all | solution.py:19
  148.1 2.6 %collective-permute-start.10 = (bf16[128,1280]{1,0:T(8,128)(2,1)}, bf16[128,1280]{1,0:T(8,128)(2,1)S(1)}, u32[]{:S(2)}, u32[]{:S(2)}) collective-permute-start(bf16[128,1280]{1,0:T(8,128)(2,1)} %get-tuple-element.55), channel_id=1, source_target_pairs={{0,12},{4,8},{8,4},{12,0},{1,13},{5,9},{9,5},{13,1},{2,14},{6,10},... | collective-permute-start | bytes 983048 | tf_op jit(solution)/shard_map/ppermute | solution.py:35
  151.8 10.4 %all-to-all-done.3 = bf16[8,16,1920]{2,1,0:T(8,128)(2,1)} async-done(((bf16[8,16,1920]{2,1,0:T(8,128)(2,1)}), bf16[8,16,1920]{2,1,0:T(8,128)(2,1)}, u32[]{:S(2)}, u32[]{:S(2)}) %all-to-all-start.3) | async-done | bytes 491552 | tf_op jit(solution)/shard_map/all_to_all | solution.py:19
  164.0 4.0 %all-to-all-start.4 = ((f32[4,16,640]{2,1,0:T(8,128)}), f32[4,16,640]{2,1,0:T(8,128)}, u32[]{:S(2)}, u32[]{:S(2)}) async-start(f32[4,16,640]{2,1,0:T(8,128)} %broadcast_in_dim.109), calls=%async_computation.4 | async-start | bytes 327680 | tf_op jit(solution)/shard_map/all_to_all | solution.py:19
  168.0 4.1 %fusion.12 = bf16[512,1280]{1,0:T(8,128)(2,1)S(1)} fusion(bf16[640,1280]{1,0:T(8,128)(2,1)} %collective-permute-done.15, bf16[640,640]{1,0:T(8,128)(2,1)} %copy-done.18, bf16[640,640]{1,0:T(8,128)(2,1)} %copy-done.17, bf16[512,640]{1,0:T(8,128)(2,1)} %copy-done.20, bf16[512,640]{1,0:T(8,128)(2,1)} %copy-done.19), kind=kOutput, calls=%fused_computation.12 | convolution fusion | flops 1690828800 | bytes 5898240 | tf_op jit(solution)/shard_map/dot_general | solution.py:87
  173.2 2.9 %collective-permute-start.16 = (bf16[128,1280]{1,0:T(8,128)(2,1)}, bf16[128,1280]{1,0:T(8,128)(2,1)}, u32[]{:S(2)}, u32[]{:S(2)}) collective-permute-start(bf16[128,1280]{1,0:T(8,128)(2,1)} %get-tuple-element.53), channel_id=1, source_target_pairs={{0,12},{4,8},{8,4},{12,0},{1,13},{5,9},{9,5},{13,1},{2,14},{6,10},... | collective-permute-start | bytes 983048 | tf_op jit(solution)/shard_map/ppermute | solution.py:35
  178.9 6.1 %collective-permute-done.16.refs_5_ = bf16[128,1280]{1,0:T(8,128)(2,1)} collective-permute-done((bf16[128,1280]{1,0:T(8,128)(2,1)}, bf16[128,1280]{1,0:T(8,128)(2,1)}, u32[]{:S(2)}, u32[]{:S(2)}) %collective-permute-start.16) | collective-permute-done | bytes 327712 | tf_op jit(solution)/shard_map/ppermute | solution.py:35
  185.0 6.4 %collective-permute-done.17.refs_6_ = bf16[128,1280]{1,0:T(8,128)(2,1)} collective-permute-done((bf16[128,1280]{1,0:T(8,128)(2,1)}, bf16[128,1280]{1,0:T(8,128)(2,1)}, u32[]{:S(2)}, u32[]{:S(2)}) %collective-permute-start.17) | collective-permute-done | bytes 327712 | tf_op jit(solution)/shard_map/ppermute | solution.py:35
  191.7 2.6 %mixed_rows.1 = bf16[128,2560]{1,0:T(8,128)(2,1)} custom-call(s32[1]{0:T(128)} %bitcast.spot, f32[128,1]{1,0:T(8,128)S(1)} %copy.25.scale, bf16[16,128]{1,0:T(8,128)(2,1)S(1)} %dynamic-slice_bitcast_fusion.8.adapter, bf16[16,2560]{1,0:T(8,128)(2,1)S(1)} %copy-done.7, bf16[128,1280]{1,0:T(8,128)(2,1)S(1)} %get-tuple-element.58.refs_0_, ...), custom_call_target="tpu_custom_call" | custom-call | tf_op jit(solution)/shard_map/mixed_rows/pallas_call | solution.py:392
  (128 shorter events, 43.0 us)
Async XLA Ops:
  0.6 9.5 %copy-start = (bf16[1280,640]{1,0:T(8,128)(2,1)S(1)}, bf16[1280,640]{1,0:T(8,128)(2,1)}, u32[]{:S(2)}) copy-start(bf16[1280,640]{1,0:T(8,128)(2,1)} %param.24) | copy-start | bytes 4915204
  4.9 32.5 %all-to-all-start = ((bf16[4,128,1664]{2,1,0:T(8,128)(2,1)}), bf16[4,128,1664]{2,1,0:T(8,128)(2,1)S(1)}, u32[]{:S(2)}, u32[]{:S(2)}) async-start(bf16[4,128,1664]{2,1,0:T(8,128)(2,1)} %shard_map.157), calls=%async_computation | async-start | bytes 3407872 | tf_op jit(solution)/shard_map/all_to_all | solution.py:19
  10.1 6.9 %copy-start.21 = (f32[4,5376]{1,0:T(4,128)S(1)}, f32[4,5376]{1,0:T(4,128)}, u32[]{:S(2)}) copy-start(f32[4,5376]{1,0:T(4,128)} %param.18) | copy-start | bytes 258052
  10.1 6.9 %slice-start = ((f32[4,5376]{1,0:T(4,128)}), f32[4,256]{1,0:T(4,128)S(1)}, s32[]{:S(2)}) async-start(f32[4,5376]{1,0:T(4,128)} %param.18), calls=%async_computation.5 | async-start | bytes 8192 | tf_op jit(solution)/shard_map/slice | solution.py:287
  10.1 33.3 %copy-start.25 = (f32[20]{0:T(128)S(1)}, f32[20]{0:T(128)}, u32[]{:S(2)}) copy-start(f32[20]{0:T(128)} %param.20) | copy-start | bytes 244
  10.2 45.0 %copy-start.24 = (f32[20]{0:T(128)S(1)}, f32[20]{0:T(128)}, u32[]{:S(2)}) copy-start(f32[20]{0:T(128)} %param.22) | copy-start | bytes 244
  11.2 21.2 %collective-permute-start.5 = (bf16[640,640]{1,0:T(8,128)(2,1)}, bf16[640,640]{1,0:T(8,128)(2,1)}, u32[]{:S(2)}, u32[]{:S(2)}) collective-permute-start(bf16[640,640]{1,0:T(8,128)(2,1)} %constant_dynamic-slice_fusion.1), channel_id=1, source_target_pairs={{0,1},{1,2},{2,3},{4,5},{5,6},{6,7},{8,9},{9,10},{10,11},{12,13},{... | collective-permute-start | bytes 2457608 | tf_op jit(solution)/shard_map/ppermute | solution.py:44
  15.6 21.8 %collective-permute-start.6 = (bf16[640,640]{1,0:T(8,128)(2,1)}, bf16[640,640]{1,0:T(8,128)(2,1)}, u32[]{:S(2)}, u32[]{:S(2)}) collective-permute-start(bf16[640,640]{1,0:T(8,128)(2,1)} %constant_dynamic-slice_fusion.1), channel_id=1, source_target_pairs={{1,0},{2,1},{3,2},{5,4},{6,5},{7,6},{9,8},{10,9},{11,10},{13,12},{... | collective-permute-start | bytes 2457608 | tf_op jit(solution)/shard_map/ppermute | solution.py:44
  37.4 30.9 %collective-permute-start.7 = (bf16[640,640]{1,0:T(8,128)(2,1)}, bf16[640,640]{1,0:T(8,128)(2,1)}, u32[]{:S(2)}, u32[]{:S(2)}) collective-permute-start(bf16[640,640]{1,0:T(8,128)(2,1)} %collective-permute-done.5), channel_id=1, source_target_pairs={{0,1},{1,2},{2,3},{4,5},{5,6},{6,7},{8,9},{9,10},{10,11},{12,13},{... | collective-permute-start | bytes 2457608 | tf_op jit(solution)/shard_map/ppermute | solution.py:44
  40.8 27.5 %collective-permute-start.8 = (bf16[640,640]{1,0:T(8,128)(2,1)}, bf16[640,640]{1,0:T(8,128)(2,1)}, u32[]{:S(2)}, u32[]{:S(2)}) collective-permute-start(bf16[640,640]{1,0:T(8,128)(2,1)} %collective-permute-done.6), channel_id=1, source_target_pairs={{1,0},{2,1},{3,2},{5,4},{6,5},{7,6},{9,8},{10,9},{11,10},{13,12},{... | collective-permute-start | bytes 2457608 | tf_op jit(solution)/shard_map/ppermute | solution.py:44
  42.1 2.1 %collective-permute-start = (bf16[8,1536]{1,0:T(8,128)(2,1)S(1)}, bf16[8,1536]{1,0:T(8,128)(2,1)S(1)}, u32[]{:S(2)}, u32[]{:S(2)}) collective-permute-start(bf16[8,1536]{1,0:T(8,128)(2,1)S(1)} %slice_bitcast_fusion.1), channel_id=1, source_target_pairs={{0,16},{1,17},{2,18},{3,19},{4,20},{5,21},{6,22},{7,23},{8,24},{9,... | collective-permute-start | bytes 73736 | tf_op jit(solution)/shard_map/ppermute | solution.py:44
  52.9 4.2 %collective-permute-start.1 = (f32[128,1280]{1,0:T(8,128)}, f32[128,1280]{1,0:T(8,128)S(1)}, u32[]{:S(2)}, u32[]{:S(2)}) collective-permute-start(f32[128,1280]{1,0:T(8,128)} %get-tuple-element.31), channel_id=1, source_target_pairs={{0,16},{1,17},{2,18},{3,19},{4,20},{5,21},{6,22},{7,23},{8,24},{9,... | collective-permute-start | bytes 1966088 | tf_op jit(solution)/shard_map/ppermute | solution.py:222
  73.6 42.1 %collective-permute-start.9 = (bf16[640,1280]{1,0:T(8,128)(2,1)}, bf16[640,1280]{1,0:T(8,128)(2,1)}, u32[]{:S(2)}, u32[]{:S(2)}) collective-permute-start(bf16[640,1280]{1,0:T(8,128)(2,1)} %pad_maximum_fusion), channel_id=1, source_target_pairs={{0,16},{16,0},{1,17},{17,1},{2,18},{18,2},{3,19},{19,3},{4,20},{20... | collective-permute-start | bytes 4915208 | tf_op jit(solution)/shard_map/ppermute | solution.py:334
  76.4 7.7 %copy-start.7 = (bf16[16,2560]{1,0:T(8,128)(2,1)S(1)}, bf16[16,2560]{1,0:T(8,128)(2,1)}, u32[]{:S(2)}) copy-start(bf16[16,2560]{1,0:T(8,128)(2,1)} %up.1) | copy-start | bytes 245764
  76.5 20.7 %all-to-all-start.1 = ((bf16[4,128,1280]{2,1,0:T(8,128)(2,1)}), bf16[4,128,1280]{2,1,0:T(8,128)(2,1)S(1)}, u32[]{:S(2)}, u32[]{:S(2)}) async-start(bf16[4,128,1280]{2,1,0:T(8,128)(2,1)} %shard_map.158), calls=%async_computation.1 | async-start | bytes 2621440 | tf_op jit(solution)/shard_map/all_to_all | solution.py:19
  80.4 17.8 %copy-start.14 = (bf16[1280,16]{0,1:T(8,128)(2,1)S(1)}, bf16[1280,16]{0,1:T(8,128)(2,1)}, u32[]{:S(2)}) copy-start(bf16[1280,16]{0,1:T(8,128)(2,1)} %param.25) | copy-start | bytes 122884
  103.3 35.9 %collective-permute-start.2 = (f32[112,128]{1,0:T(8,128)S(1)}, f32[112,128]{1,0:T(8,128)S(1)}, u32[]{:S(2)}, u32[]{:S(2)}) collective-permute-start(f32[112,128]{1,0:T(8,128)S(1)} %pad_maximum_fusion.6), channel_id=1, source_target_pairs={{0,4},{4,0},{8,12},{12,8},{1,5},{5,1},{9,13},{13,9},{2,6},{6,2},{1... | collective-permute-start | bytes 172040 | tf_op jit(solution)/shard_map/ppermute | solution.py:35
  104.8 34.4 %collective-permute-start.3 = (f32[112,128]{1,0:T(8,128)S(1)}, f32[112,128]{1,0:T(8,128)}, u32[]{:S(2)}, u32[]{:S(2)}) collective-permute-start(f32[112,128]{1,0:T(8,128)S(1)} %pad_maximum_fusion.6), channel_id=1, source_target_pairs={{0,8},{4,12},{8,0},{12,4},{1,9},{5,13},{9,1},{13,5},{2,10},{6,14},... | collective-permute-start | bytes 172040 | tf_op jit(solution)/shard_map/ppermute | solution.py:35
  105.4 35.4 %all-to-all-start.2 = ((bf16[4,128,640]{2,1,0:T(8,128)(2,1)}), bf16[4,128,640]{2,1,0:T(8,128)(2,1)}, u32[]{:S(2)}, u32[]{:S(2)}) async-start(bf16[4,128,640]{2,1,0:T(8,128)(2,1)} %shard_map.159), calls=%async_computation.2 | async-start | bytes 1310720 | tf_op jit(solution)/shard_map/all_to_all | solution.py:19
  109.5 9.1 %copy-start.16 = (bf16[640,640]{1,0:T(8,128)(2,1)S(1)}, bf16[640,640]{1,0:T(8,128)(2,1)}, u32[]{:S(2)}) copy-start(bf16[640,640]{1,0:T(8,128)(2,1)} %copy-done.15) | copy-start | bytes 2457604
  109.5 21.1 %collective-permute-start.13 = (bf16[640,640]{1,0:T(8,128)(2,1)}, bf16[640,640]{1,0:T(8,128)(2,1)S(1)}, u32[]{:S(2)}, u32[]{:S(2)}) collective-permute-start(bf16[640,640]{1,0:T(8,128)(2,1)} %collective-permute-done.7), channel_id=1, source_target_pairs={{0,1},{1,2},{2,3},{4,5},{5,6},{6,7},{8,9},{9,10},{10,11},{12,13},{... | collective-permute-start | bytes 2457608 | tf_op jit(solution)/shard_map/ppermute | solution.py:44
  114.3 20.5 %collective-permute-start.14 = (bf16[640,640]{1,0:T(8,128)(2,1)}, bf16[640,640]{1,0:T(8,128)(2,1)S(1)}, u32[]{:S(2)}, u32[]{:S(2)}) collective-permute-start(bf16[640,640]{1,0:T(8,128)(2,1)} %collective-permute-done.8), channel_id=1, source_target_pairs={{1,0},{2,1},{3,2},{5,4},{6,5},{7,6},{9,8},{10,9},{11,10},{13,12},{... | collective-permute-start | bytes 2457608 | tf_op jit(solution)/shard_map/ppermute | solution.py:44
  115.7 23.5 %collective-permute-start.4 = (f32[112,128]{1,0:T(8,128)S(1)}, f32[112,128]{1,0:T(8,128)S(1)}, u32[]{:S(2)}, u32[]{:S(2)}) collective-permute-start(f32[112,128]{1,0:T(8,128)S(1)} %pad_maximum_fusion.6), channel_id=1, source_target_pairs={{0,12},{4,8},{8,4},{12,0},{1,13},{5,9},{9,5},{13,1},{2,14},{6,10},... | collective-permute-start | bytes 172040 | tf_op jit(solution)/shard_map/ppermute | solution.py:35
  139.9 28.1 %collective-permute-start.15 = (bf16[640,1280]{1,0:T(8,128)(2,1)}, bf16[640,1280]{1,0:T(8,128)(2,1)}, u32[]{:S(2)}, u32[]{:S(2)}) collective-permute-start(bf16[640,1280]{1,0:T(8,128)(2,1)} %pad_maximum_fusion.1), channel_id=1, source_target_pairs={{0,16},{16,0},{1,17},{17,1},{2,18},{18,2},{3,19},{19,3},{4,20},{20... | collective-permute-start | bytes 4915208 | tf_op jit(solution)/shard_map/ppermute | solution.py:334
  144.0 18.2 %all-to-all-start.3 = ((bf16[8,16,1920]{2,1,0:T(8,128)(2,1)}), bf16[8,16,1920]{2,1,0:T(8,128)(2,1)}, u32[]{:S(2)}, u32[]{:S(2)}) async-start(bf16[8,16,1920]{2,1,0:T(8,128)(2,1)} %broadcast_in_dim.108), calls=%async_computation.3 | async-start | bytes 983040 | tf_op jit(solution)/shard_map/all_to_all | solution.py:19
  148.1 28.5 %collective-permute-start.10 = (bf16[128,1280]{1,0:T(8,128)(2,1)}, bf16[128,1280]{1,0:T(8,128)(2,1)S(1)}, u32[]{:S(2)}, u32[]{:S(2)}) collective-permute-start(bf16[128,1280]{1,0:T(8,128)(2,1)} %get-tuple-element.55), channel_id=1, source_target_pairs={{0,12},{4,8},{8,4},{12,0},{1,13},{5,9},{9,5},{13,1},{2,14},{6,10},... | collective-permute-start | bytes 983048 | tf_op jit(solution)/shard_map/ppermute | solution.py:35
  150.8 28.1 %collective-permute-start.11 = (bf16[128,1280]{1,0:T(8,128)(2,1)}, bf16[128,1280]{1,0:T(8,128)(2,1)S(1)}, u32[]{:S(2)}, u32[]{:S(2)}) collective-permute-start(bf16[128,1280]{1,0:T(8,128)(2,1)} %get-tuple-element.56), channel_id=1, source_target_pairs={{0,8},{4,12},{8,0},{12,4},{1,9},{5,13},{9,1},{13,5},{2,10},{6,14},... | collective-permute-start | bytes 983048 | tf_op jit(solution)/shard_map/ppermute | solution.py:35
  151.3 27.6 %collective-permute-start.12 = (bf16[128,1280]{1,0:T(8,128)(2,1)}, bf16[128,1280]{1,0:T(8,128)(2,1)S(1)}, u32[]{:S(2)}, u32[]{:S(2)}) collective-permute-start(bf16[128,1280]{1,0:T(8,128)(2,1)} %get-tuple-element.57), channel_id=1, source_target_pairs={{0,4},{4,0},{8,12},{12,8},{1,5},{5,1},{9,13},{13,9},{2,6},{6,2},{1... | collective-permute-start | bytes 983048 | tf_op jit(solution)/shard_map/ppermute | solution.py:35
  164.0 13.3 %all-to-all-start.4 = ((f32[4,16,640]{2,1,0:T(8,128)}), f32[4,16,640]{2,1,0:T(8,128)}, u32[]{:S(2)}, u32[]{:S(2)}) async-start(f32[4,16,640]{2,1,0:T(8,128)} %broadcast_in_dim.109), calls=%async_computation.4 | async-start | bytes 327680 | tf_op jit(solution)/shard_map/all_to_all | solution.py:19
  173.2 11.8 %collective-permute-start.16 = (bf16[128,1280]{1,0:T(8,128)(2,1)}, bf16[128,1280]{1,0:T(8,128)(2,1)}, u32[]{:S(2)}, u32[]{:S(2)}) collective-permute-start(bf16[128,1280]{1,0:T(8,128)(2,1)} %get-tuple-element.53), channel_id=1, source_target_pairs={{0,12},{4,8},{8,4},{12,0},{1,13},{5,9},{9,5},{13,1},{2,14},{6,10},... | collective-permute-start | bytes 983048 | tf_op jit(solution)/shard_map/ppermute | solution.py:35
  176.0 15.4 %collective-permute-start.17 = (bf16[128,1280]{1,0:T(8,128)(2,1)}, bf16[128,1280]{1,0:T(8,128)(2,1)}, u32[]{:S(2)}, u32[]{:S(2)}) collective-permute-start(bf16[128,1280]{1,0:T(8,128)(2,1)} %get-tuple-element.52), channel_id=1, source_target_pairs={{0,8},{4,12},{8,0},{12,4},{1,9},{5,13},{9,1},{13,5},{2,10},{6,14},... | collective-permute-start | bytes 983048 | tf_op jit(solution)/shard_map/ppermute | solution.py:35
  176.6 15.1 %collective-permute-start.18 = (bf16[128,1280]{1,0:T(8,128)(2,1)}, bf16[128,1280]{1,0:T(8,128)(2,1)}, u32[]{:S(2)}, u32[]{:S(2)}) collective-permute-start(bf16[128,1280]{1,0:T(8,128)(2,1)} %get-tuple-element.51), channel_id=1, source_target_pairs={{0,4},{4,0},{8,12},{12,8},{1,5},{5,1},{9,13},{13,9},{2,6},{6,2},{1... | collective-permute-start | bytes 983048 | tf_op jit(solution)/shard_map/ppermute | solution.py:35
  (21 other events, 61.7 us)
